TPU v7x, 256 devices: a whole 4x4x8 slice. The times are simulated.
256 devices in a mesh: dp: 8 (over x, core), band: 32 (over y, z).
Axes of the slice: x: 4, y: 4, z: 8, core: 2. Of those that a mesh axis runs over, the one named last changes fastest.
Arguments:
- features: bfloat16 [65280, 256], P(('dp', 'band')), parts along dimension 0, may hold values from -6 to 6
- corners: int32 [65280, 512], P(('dp', 'band')), parts along dimension 0, may hold values from 0 to 6143, as said below
- bilinear: float32 [65280, 512], P(('dp', 'band')), parts along dimension 0, may hold values from 0.08 to 0.5, as said below
- attention: float32 [65280, 128], P(('dp', 'band')), parts along dimension 0, may hold values from 0 to 1, as said below
- w_value: bfloat16 [256, 256], replicated, may hold values from -0.375 to 0.375
- b_value: float32 [256], replicated, may hold values from -0.6 to 0.6
- w_out: bfloat16 [256, 256], replicated, may hold values from -1.5 to 1.5
- b_out: float32 [256], replicated, may hold values from -3 to 3
- norm1_gain: float32 [256], replicated, may hold values from 0.5 to 1.5
- norm1_bias: float32 [256], replicated, may hold values from -3 to 3
- w_in: bfloat16 [256, 1024], replicated, may hold values from -0.375 to 0.375
- b_in: float32 [1024], replicated, may hold values from -3 to 3
- w_ffout: bfloat16 [1024, 256], replicated, may hold values from -0.1875 to 0.1875
- b_ffout: float32 [256], replicated, may hold values from -3 to 3
- norm2_gain: float32 [256], replicated, may hold values from 0.5 to 1.5
- norm2_bias: float32 [256], replicated, may hold values from -3 to 3
Outputs:
- encoded: bfloat16 [65280, 256], P(('dp', 'band')), parts along dimension 0
There are 8 independent parts, one for each index of `dp`. A program takes and returns all parts, laid end to end along the dimension named above; an argument that names none is the same for every part. Nothing has to cross between parts.
Inputs may be any that keep to these rules, and one draw needn't show every extreme that they name: An entry for level l is a row of a map of 192 * 32 // 4**l tokens laid out in rows of 128 // 2**l; the four corners of a point are k, k + 1, k + 128 // 2**l and k + 128 // 2**l + 1 in that order. `bilinear`: the four corner weights of a point are positive and sum to one. `attention`: for each token and head the 16 weights are positive and sum to one.
All inputs are finite; a program needn't handle non-finite values.
Results may differ from a plain program's by a relative error of at most 0.009.
Values may be sent and summed in bfloat16 or wider, within the bound.
A program may use at most 64 MiB of HBM per device.

v0:
```python
import jax
import jax.numpy as jnp
from jax import lax
from jax.sharding import Mesh
from jax.sharding import PartitionSpec as P

HEADS = 8
LEVELS = 4
POINTS = 4
ROWS_DEV = 192
BAND = ("band_0", "band_1")
DP_BAND = ("dp", "band_0", "band_1")


def joined_along(pieces, dim):
    pieces = jnp.moveaxis(pieces, 0, dim)
    dims = pieces.shape
    return pieces.reshape(*dims[:dim], dims[dim] * dims[dim + 1], *dims[dim + 2 :])


def stacked_from(shard, axes, order):
    pieces = shard[None]
    for k in order:
        pieces = lax.all_gather(pieces, axes[k], axis=0, tiled=True)
    held = [lax.axis_size(axes[k]) for k in reversed(order)]
    pieces = pieces.reshape(*held, *shard.shape)
    turned = sorted(range(len(order)), key=lambda place: order[len(order) - 1 - place])
    return pieces.transpose(*turned, *range(len(order), pieces.ndim)).reshape(-1, *shard.shape)


def gathered_by_axis(shard, axes, order, dim):
    return joined_along(stacked_from(shard, axes, order), dim)


def layer_norm(inputs, gain, shift):
    average = jnp.mean(inputs, axis=-1, keepdims=True)
    centred = inputs - average
    variance = jnp.mean(centred * centred, axis=-1, keepdims=True)
    return centred * lax.rsqrt(variance + 1e-05) * gain + shift


def blend_rows(place_heads, weight_heads, value_block):
    row_count, model_width = value_block.shape
    head_dim = model_width // HEADS
    lane_groups = -(-row_count // 128)
    padding = lane_groups * 128 - row_count
    padded = jnp.pad(value_block, ((0, padding), (0, 0))).reshape(lane_groups, 128, HEADS, head_dim)
    per_head = jnp.transpose(padded, (2, 0, 1, 3))
    group_ids = jnp.arange(lane_groups, dtype=jnp.int32)
    lane_ids = jnp.arange(128, dtype=jnp.int32)

    def one_head(head_args):
        place_one, weight_one, value_one = head_args
        group_index = place_one // 128
        lane_index = place_one % 128
        group_hits = jnp.where(
            group_index[..., None] == group_ids, weight_one[..., None], jnp.zeros((), jnp.bfloat16)
        )
        lane_hits = (lane_index[..., None] == lane_ids).astype(jnp.bfloat16)
        hit_table = jnp.einsum(
            "qsa,qsb->qab", group_hits, lane_hits, preferred_element_type=jnp.float32
        )
        table_major = hit_table.astype(jnp.bfloat16)
        table_minor = (hit_table - table_major.astype(jnp.float32)).astype(jnp.bfloat16)
        result_major = jnp.einsum(
            "qab,abd->qd", table_major, value_one, preferred_element_type=jnp.float32
        )
        result_minor = jnp.einsum(
            "qab,abd->qd", table_minor, value_one, preferred_element_type=jnp.float32
        )
        return result_major + result_minor

    blended = lax.map(one_head, (place_heads, weight_heads, per_head))
    return jnp.transpose(blended, (1, 0, 2))


def body(
    features,
    corners,
    bilinear,
    attention,
    w_value,
    b_value,
    w_out,
    b_out,
    norm1_gain,
    norm1_bias,
    w_in,
    b_in,
    w_ffout,
    b_ffout,
    norm2_gain,
    norm2_bias,
):
    band_rows, model_width = features.shape
    samples = LEVELS * POINTS * 4
    segment_rows = [ROWS_DEV // 4**level_index for level_index in range(LEVELS)]
    segment_start = [sum(segment_rows[:level_index]) for level_index in range(LEVELS)]
    value_rows = (jnp.dot(features, w_value, preferred_element_type=jnp.float32) + b_value).astype(
        jnp.bfloat16
    )
    weight = (
        attention.reshape(band_rows, HEADS, LEVELS, POINTS, 1)
        * bilinear.reshape(band_rows, HEADS, LEVELS, POINTS, 4)
    ).astype(jnp.bfloat16)
    weight_heads = jnp.transpose(weight.reshape(band_rows, HEADS, samples), (1, 0, 2))
    corner_table = corners.reshape(band_rows, HEADS, LEVELS, POINTS * 4)
    places = []
    for level_index in range(LEVELS):
        level_corner = corner_table[:, :, level_index]
        places.append(
            level_corner // segment_rows[level_index] * band_rows
            + segment_start[level_index]
            + level_corner % segment_rows[level_index]
        )
    place_table = jnp.stack(places, axis=2).reshape(band_rows, HEADS, samples)
    place_heads = jnp.transpose(place_table, (1, 0, 2))
    whole = gathered_by_axis(value_rows, BAND, (0, 1), 0)
    running_sum = blend_rows(place_heads, weight_heads, whole)
    sampled = running_sum.reshape(band_rows, model_width).astype(jnp.bfloat16)
    attended = jnp.dot(sampled, w_out, preferred_element_type=jnp.float32) + b_out
    middle = layer_norm(features.astype(jnp.float32) + attended, norm1_gain, norm1_bias).astype(
        jnp.bfloat16
    )
    hidden = jnp.maximum(
        jnp.dot(middle, w_in, preferred_element_type=jnp.float32) + b_in, 0.0
    ).astype(jnp.bfloat16)
    result = (
        middle.astype(jnp.float32)
        + jnp.dot(hidden, w_ffout, preferred_element_type=jnp.float32)
        + b_ffout
    )
    return layer_norm(result, norm2_gain, norm2_bias).astype(jnp.bfloat16)


def solution(mesh):
    split = Mesh(mesh.devices.reshape(mesh.shape["dp"], 4, 8), ("dp", "band_0", "band_1"))
    return jax.shard_map(
        body,
        mesh=split,
        in_specs=(
            P(DP_BAND, None),
            P(DP_BAND, None),
            P(DP_BAND, None),
            P(DP_BAND, None),
            P(),
            P(),
            P(),
            P(),
            P(),
            P(),
            P(),
            P(),
            P(),
            P(),
            P(),
            P(),
        ),
        out_specs=P(DP_BAND, None),
        check_vma=False,
    )
```

profile of v0, /device:TPU:6, one launch (start us, length us, event | category | flops | bytes accessed | tf_op | source)
XLA Modules:
  0.0 195.5 jit_solution(10287885254114032804)
XLA Ops:
  6.5 1.2 fusion.41
  7.8 14.0 %all-gather.1 = bf16[4,255,256]{2,1,0:T(8,128)(2,1)} all-gather(bf16[1,255,256]{2,1,0:T(8,128)(2,1)S(1)} %fusion.41), channel_id=2, replica_groups=mesh['dp'=8,'band_0'=4,'band_1'=8] {'band_0'}, dimensions={0}, use_global_device_ids=true | all-gather | bytes 652800 | tf_op jit(solution)/shard_map/all_gather | solution.py:24
  21.8 1.2 copy.38
  23.1 1.2 copy.41
  24.3 1.0 copy.39
  25.8 0.5 fusion.46
  26.4 53.2 %all-gather.4.cloned.1.call-done = bf16[32,255,256]{2,1,0:T(8,128)(2,1)} async-done(((bf16[4,255,256]{2,1,0:T(8,128)(2,1)}), bf16[32,255,256]{2,1,0:T(8,128)(2,1)}) %all-gather.4.cloned.1.call-update) | async-done | bytes 4177936 | tf_op jit(solution)/shard_map/all_gather | solution.py:24
  79.6 4.6 %copy.72 = bf16[8,4,255,256]{3,2,0,1:T(8,128)(2,1)} copy(bf16[8,4,255,256]{3,2,1,0:T(8,128)(2,1)} %bitcast.96) | data formatting | bytes 8355840 | tf_op jit(solution)/shard_map/reshape | solution.py:26
  84.2 5.2 %reshape_reshape.3 = bf16[8160,256]{1,0:T(8,128)(2,1)} reshape(bf16[4,8,255,256]{3,2,1,0:T(8,128)(2,1)} %bitcast.94) | data formatting | bytes 8355840 | tf_op jit(solution)/shard_map/reshape;reshape | solution.py:18
  89.4 6.4 %copy.51 = bf16[8160,256]{0,1:T(8,128)(2,1)} copy(bf16[8160,256]{1,0:T(8,128)(2,1)} %reshape_reshape.3) | data formatting | bytes 8355840
  95.8 2.5 %pad_bitcast_fusion = bf16[32,8,64,128]{3,1,2,0:T(8,128)(2,1)S(1)} fusion(bf16[8160,256]{0,1:T(8,128)(2,1)} %copy.51), kind=kLoop, calls=%fused_computation.35 | loop fusion | bytes 8372224
  98.3 3.1 %copy.52 = bf16[32,8,64,128]{3,2,1,0:T(8,128)(2,1)} copy(bf16[32,8,64,128]{3,1,2,0:T(8,128)(2,1)S(1)} %pad_bitcast_fusion) | data formatting | bytes 8388608
  101.5 84.8 %while.13 = (s32[]{:T(128)}, bf16[8,255,32]{1,2,0:T(8,128)(2,1)S(1)}, s32[8,255,64]{1,2,0:T(8,128)S(1)}, bf16[8,255,64]{1,0,2:T(8,128)(2,1)S(1)}, bf16[8,64,128,32]{2,1,3,0:T(8,128)(2,1)}, /*index=5*/s32[]{:T(128)}) while((s32[]{:T(128)}, bf16[8,255,32]{1,2,0:T(8,128)(2,1)S(1)}, s32[8,255,64]{1,2,0:T(8,128)S(1)}, ...), condition=%wide.region_1.2_spmd.clone, body=%wide.region_0.1_spmd.clone.sunk | while | flops 547625728 | bytes 19657812 | solution.py:73
  102.0 4.0 %subtract_convert_fusion.2 = (bf16[255,64,128]{2,1,0:T(8,128)(2,1)S(1)}, bf16[255,64,128]{2,1,0:T(8,128)(2,1)S(1)}) fusion(s32[255,64]{1,0:T(8,128)S(1)} %get-tuple-element.178, s32[255,64]{1,0:T(8,128)S(1)} %get-tuple-element.179, bf16[255,64]{1,0:T(8,128)(2,1)S(1)} %bitcast.99), kind=kOutput, calls=%fused_computation.4.clone.1 | convolution fusion | flops 279920640 | bytes 8519040 | tf_op jit(solution)/shard_map/while/body/eval_jaxpr/qsa,qsb->qab/dot_general | solution.py:60
  105.9 1.1 constant_dynamic-slice_fusion.8
  107.0 2.5 %fusion.83 = f32[255,32]{0,1:T(8,128)S(1)} fusion(bf16[255,64,128]{2,1,0:T(8,128)(2,1)S(1)} %get-tuple-element.180, bf16[1,64,128,32]{2,1,3,0:T(8,128)(2,1)S(1)} %constant_dynamic-slice_fusion.8), kind=kOutput, calls=%fused_computation.15.clone.1 | convolution fusion | flops 133693440 | bytes 4734848 | tf_op jit(solution)/shard_map/while/body/eval_jaxpr/qab,abd->qd/dot_general | solution.py:65
  109.5 2.5 %fusion.84 = bf16[8,255,32]{1,2,0:T(8,128)(2,1)S(1)} fusion(bf16[8,255,32]{1,2,0:T(8,128)(2,1)S(1)} %get-tuple-element.189, s32[]{:T(128)} %get-tuple-element.188, f32[255,32]{0,1:T(8,128)S(1)} %fusion.83, bf16[255,64,128]{2,1,0:T(8,128)(2,1)S(1)} %get-tuple-element.181, bf16[1,64,128,32]{2,1,3,0:T(8,128)(2,1)S(1)} %constant_dynamic-slice_fusion.8), kind=kOutput, calls=%fused_computation.19.clone.1 | convolution fusion | flops 133701600 | bytes 4767748 | tf_op jit(solution)/shard_map/while/body/eval_jaxpr/qab,abd->qd/dot_general | solution.py:68
  112.6 4.0 %subtract_convert_fusion.2 = (bf16[255,64,128]{2,1,0:T(8,128)(2,1)S(1)}, bf16[255,64,128]{2,1,0:T(8,128)(2,1)S(1)}) fusion(s32[255,64]{1,0:T(8,128)S(1)} %get-tuple-element.178, s32[255,64]{1,0:T(8,128)S(1)} %get-tuple-element.179, bf16[255,64]{1,0:T(8,128)(2,1)S(1)} %bitcast.99), kind=kOutput, calls=%fused_computation.4.clone.1 | convolution fusion | flops 279920640 | bytes 8519040 | tf_op jit(solution)/shard_map/while/body/eval_jaxpr/qsa,qsb->qab/dot_general | solution.py:60
  116.5 1.1 constant_dynamic-slice_fusion.8
  117.6 2.5 %fusion.83 = f32[255,32]{0,1:T(8,128)S(1)} fusion(bf16[255,64,128]{2,1,0:T(8,128)(2,1)S(1)} %get-tuple-element.180, bf16[1,64,128,32]{2,1,3,0:T(8,128)(2,1)S(1)} %constant_dynamic-slice_fusion.8), kind=kOutput, calls=%fused_computation.15.clone.1 | convolution fusion | flops 133693440 | bytes 4734848 | tf_op jit(solution)/shard_map/while/body/eval_jaxpr/qab,abd->qd/dot_general | solution.py:65
  120.1 2.5 %fusion.84 = bf16[8,255,32]{1,2,0:T(8,128)(2,1)S(1)} fusion(bf16[8,255,32]{1,2,0:T(8,128)(2,1)S(1)} %get-tuple-element.189, s32[]{:T(128)} %get-tuple-element.188, f32[255,32]{0,1:T(8,128)S(1)} %fusion.83, bf16[255,64,128]{2,1,0:T(8,128)(2,1)S(1)} %get-tuple-element.181, bf16[1,64,128,32]{2,1,3,0:T(8,128)(2,1)S(1)} %constant_dynamic-slice_fusion.8), kind=kOutput, calls=%fused_computation.19.clone.1 | convolution fusion | flops 133701600 | bytes 4767748 | tf_op jit(solution)/shard_map/while/body/eval_jaxpr/qab,abd->qd/dot_general | solution.py:68
  123.2 4.0 %subtract_convert_fusion.2 = (bf16[255,64,128]{2,1,0:T(8,128)(2,1)S(1)}, bf16[255,64,128]{2,1,0:T(8,128)(2,1)S(1)}) fusion(s32[255,64]{1,0:T(8,128)S(1)} %get-tuple-element.178, s32[255,64]{1,0:T(8,128)S(1)} %get-tuple-element.179, bf16[255,64]{1,0:T(8,128)(2,1)S(1)} %bitcast.99), kind=kOutput, calls=%fused_computation.4.clone.1 | convolution fusion | flops 279920640 | bytes 8519040 | tf_op jit(solution)/shard_map/while/body/eval_jaxpr/qsa,qsb->qab/dot_general | solution.py:60
  127.1 1.1 constant_dynamic-slice_fusion.8
  128.2 2.5 %fusion.83 = f32[255,32]{0,1:T(8,128)S(1)} fusion(bf16[255,64,128]{2,1,0:T(8,128)(2,1)S(1)} %get-tuple-element.180, bf16[1,64,128,32]{2,1,3,0:T(8,128)(2,1)S(1)} %constant_dynamic-slice_fusion.8), kind=kOutput, calls=%fused_computation.15.clone.1 | convolution fusion | flops 133693440 | bytes 4734848 | tf_op jit(solution)/shard_map/while/body/eval_jaxpr/qab,abd->qd/dot_general | solution.py:65
  130.7 2.5 %fusion.84 = bf16[8,255,32]{1,2,0:T(8,128)(2,1)S(1)} fusion(bf16[8,255,32]{1,2,0:T(8,128)(2,1)S(1)} %get-tuple-element.189, s32[]{:T(128)} %get-tuple-element.188, f32[255,32]{0,1:T(8,128)S(1)} %fusion.83, bf16[255,64,128]{2,1,0:T(8,128)(2,1)S(1)} %get-tuple-element.181, bf16[1,64,128,32]{2,1,3,0:T(8,128)(2,1)S(1)} %constant_dynamic-slice_fusion.8), kind=kOutput, calls=%fused_computation.19.clone.1 | convolution fusion | flops 133701600 | bytes 4767748 | tf_op jit(solution)/shard_map/while/body/eval_jaxpr/qab,abd->qd/dot_general | solution.py:68
  133.8 3.9 %subtract_convert_fusion.2 = (bf16[255,64,128]{2,1,0:T(8,128)(2,1)S(1)}, bf16[255,64,128]{2,1,0:T(8,128)(2,1)S(1)}) fusion(s32[255,64]{1,0:T(8,128)S(1)} %get-tuple-element.178, s32[255,64]{1,0:T(8,128)S(1)} %get-tuple-element.179, bf16[255,64]{1,0:T(8,128)(2,1)S(1)} %bitcast.99), kind=kOutput, calls=%fused_computation.4.clone.1 | convolution fusion | flops 279920640 | bytes 8519040 | tf_op jit(solution)/shard_map/while/body/eval_jaxpr/qsa,qsb->qab/dot_general | solution.py:60
  137.7 1.1 constant_dynamic-slice_fusion.8
  138.8 2.5 %fusion.83 = f32[255,32]{0,1:T(8,128)S(1)} fusion(bf16[255,64,128]{2,1,0:T(8,128)(2,1)S(1)} %get-tuple-element.180, bf16[1,64,128,32]{2,1,3,0:T(8,128)(2,1)S(1)} %constant_dynamic-slice_fusion.8), kind=kOutput, calls=%fused_computation.15.clone.1 | convolution fusion | flops 133693440 | bytes 4734848 | tf_op jit(solution)/shard_map/while/body/eval_jaxpr/qab,abd->qd/dot_general | solution.py:65
  141.3 2.5 %fusion.84 = bf16[8,255,32]{1,2,0:T(8,128)(2,1)S(1)} fusion(bf16[8,255,32]{1,2,0:T(8,128)(2,1)S(1)} %get-tuple-element.189, s32[]{:T(128)} %get-tuple-element.188, f32[255,32]{0,1:T(8,128)S(1)} %fusion.83, bf16[255,64,128]{2,1,0:T(8,128)(2,1)S(1)} %get-tuple-element.181, bf16[1,64,128,32]{2,1,3,0:T(8,128)(2,1)S(1)} %constant_dynamic-slice_fusion.8), kind=kOutput, calls=%fused_computation.19.clone.1 | convolution fusion | flops 133701600 | bytes 4767748 | tf_op jit(solution)/shard_map/while/body/eval_jaxpr/qab,abd->qd/dot_general | solution.py:68
  144.4 4.0 %subtract_convert_fusion.2 = (bf16[255,64,128]{2,1,0:T(8,128)(2,1)S(1)}, bf16[255,64,128]{2,1,0:T(8,128)(2,1)S(1)}) fusion(s32[255,64]{1,0:T(8,128)S(1)} %get-tuple-element.178, s32[255,64]{1,0:T(8,128)S(1)} %get-tuple-element.179, bf16[255,64]{1,0:T(8,128)(2,1)S(1)} %bitcast.99), kind=kOutput, calls=%fused_computation.4.clone.1 | convolution fusion | flops 279920640 | bytes 8519040 | tf_op jit(solution)/shard_map/while/body/eval_jaxpr/qsa,qsb->qab/dot_general | solution.py:60
  148.3 1.1 constant_dynamic-slice_fusion.8
  149.4 2.5 %fusion.83 = f32[255,32]{0,1:T(8,128)S(1)} fusion(bf16[255,64,128]{2,1,0:T(8,128)(2,1)S(1)} %get-tuple-element.180, bf16[1,64,128,32]{2,1,3,0:T(8,128)(2,1)S(1)} %constant_dynamic-slice_fusion.8), kind=kOutput, calls=%fused_computation.15.clone.1 | convolution fusion | flops 133693440 | bytes 4734848 | tf_op jit(solution)/shard_map/while/body/eval_jaxpr/qab,abd->qd/dot_general | solution.py:65
  152.0 2.5 %fusion.84 = bf16[8,255,32]{1,2,0:T(8,128)(2,1)S(1)} fusion(bf16[8,255,32]{1,2,0:T(8,128)(2,1)S(1)} %get-tuple-element.189, s32[]{:T(128)} %get-tuple-element.188, f32[255,32]{0,1:T(8,128)S(1)} %fusion.83, bf16[255,64,128]{2,1,0:T(8,128)(2,1)S(1)} %get-tuple-element.181, bf16[1,64,128,32]{2,1,3,0:T(8,128)(2,1)S(1)} %constant_dynamic-slice_fusion.8), kind=kOutput, calls=%fused_computation.19.clone.1 | convolution fusion | flops 133701600 | bytes 4767748 | tf_op jit(solution)/shard_map/while/body/eval_jaxpr/qab,abd->qd/dot_general | solution.py:68
  155.0 3.9 %subtract_convert_fusion.2 = (bf16[255,64,128]{2,1,0:T(8,128)(2,1)S(1)}, bf16[255,64,128]{2,1,0:T(8,128)(2,1)S(1)}) fusion(s32[255,64]{1,0:T(8,128)S(1)} %get-tuple-element.178, s32[255,64]{1,0:T(8,128)S(1)} %get-tuple-element.179, bf16[255,64]{1,0:T(8,128)(2,1)S(1)} %bitcast.99), kind=kOutput, calls=%fused_computation.4.clone.1 | convolution fusion | flops 279920640 | bytes 8519040 | tf_op jit(solution)/shard_map/while/body/eval_jaxpr/qsa,qsb->qab/dot_general | solution.py:60
  158.9 1.1 constant_dynamic-slice_fusion.8
  160.0 2.5 %fusion.83 = f32[255,32]{0,1:T(8,128)S(1)} fusion(bf16[255,64,128]{2,1,0:T(8,128)(2,1)S(1)} %get-tuple-element.180, bf16[1,64,128,32]{2,1,3,0:T(8,128)(2,1)S(1)} %constant_dynamic-slice_fusion.8), kind=kOutput, calls=%fused_computation.15.clone.1 | convolution fusion | flops 133693440 | bytes 4734848 | tf_op jit(solution)/shard_map/while/body/eval_jaxpr/qab,abd->qd/dot_general | solution.py:65
  162.6 2.5 %fusion.84 = bf16[8,255,32]{1,2,0:T(8,128)(2,1)S(1)} fusion(bf16[8,255,32]{1,2,0:T(8,128)(2,1)S(1)} %get-tuple-element.189, s32[]{:T(128)} %get-tuple-element.188, f32[255,32]{0,1:T(8,128)S(1)} %fusion.83, bf16[255,64,128]{2,1,0:T(8,128)(2,1)S(1)} %get-tuple-element.181, bf16[1,64,128,32]{2,1,3,0:T(8,128)(2,1)S(1)} %constant_dynamic-slice_fusion.8), kind=kOutput, calls=%fused_computation.19.clone.1 | convolution fusion | flops 133701600 | bytes 4767748 | tf_op jit(solution)/shard_map/while/body/eval_jaxpr/qab,abd->qd/dot_general | solution.py:68
  165.6 4.0 %subtract_convert_fusion.2 = (bf16[255,64,128]{2,1,0:T(8,128)(2,1)S(1)}, bf16[255,64,128]{2,1,0:T(8,128)(2,1)S(1)}) fusion(s32[255,64]{1,0:T(8,128)S(1)} %get-tuple-element.178, s32[255,64]{1,0:T(8,128)S(1)} %get-tuple-element.179, bf16[255,64]{1,0:T(8,128)(2,1)S(1)} %bitcast.99), kind=kOutput, calls=%fused_computation.4.clone.1 | convolution fusion | flops 279920640 | bytes 8519040 | tf_op jit(solution)/shard_map/while/body/eval_jaxpr/qsa,qsb->qab/dot_general | solution.py:60
  169.5 1.1 constant_dynamic-slice_fusion.8
  170.6 2.5 %fusion.83 = f32[255,32]{0,1:T(8,128)S(1)} fusion(bf16[255,64,128]{2,1,0:T(8,128)(2,1)S(1)} %get-tuple-element.180, bf16[1,64,128,32]{2,1,3,0:T(8,128)(2,1)S(1)} %constant_dynamic-slice_fusion.8), kind=kOutput, calls=%fused_computation.15.clone.1 | convolution fusion | flops 133693440 | bytes 4734848 | tf_op jit(solution)/shard_map/while/body/eval_jaxpr/qab,abd->qd/dot_general | solution.py:65
  173.2 2.5 %fusion.84 = bf16[8,255,32]{1,2,0:T(8,128)(2,1)S(1)} fusion(bf16[8,255,32]{1,2,0:T(8,128)(2,1)S(1)} %get-tuple-element.189, s32[]{:T(128)} %get-tuple-element.188, f32[255,32]{0,1:T(8,128)S(1)} %fusion.83, bf16[255,64,128]{2,1,0:T(8,128)(2,1)S(1)} %get-tuple-element.181, bf16[1,64,128,32]{2,1,3,0:T(8,128)(2,1)S(1)} %constant_dynamic-slice_fusion.8), kind=kOutput, calls=%fused_computation.19.clone.1 | convolution fusion | flops 133701600 | bytes 4767748 | tf_op jit(solution)/shard_map/while/body/eval_jaxpr/qab,abd->qd/dot_general | solution.py:68
  176.2 4.0 %subtract_convert_fusion.2 = (bf16[255,64,128]{2,1,0:T(8,128)(2,1)S(1)}, bf16[255,64,128]{2,1,0:T(8,128)(2,1)S(1)}) fusion(s32[255,64]{1,0:T(8,128)S(1)} %get-tuple-element.178, s32[255,64]{1,0:T(8,128)S(1)} %get-tuple-element.179, bf16[255,64]{1,0:T(8,128)(2,1)S(1)} %bitcast.99), kind=kOutput, calls=%fused_computation.4.clone.1 | convolution fusion | flops 279920640 | bytes 8519040 | tf_op jit(solution)/shard_map/while/body/eval_jaxpr/qsa,qsb->qab/dot_general | solution.py:60
  180.1 1.1 constant_dynamic-slice_fusion.8
  181.2 2.5 %fusion.83 = f32[255,32]{0,1:T(8,128)S(1)} fusion(bf16[255,64,128]{2,1,0:T(8,128)(2,1)S(1)} %get-tuple-element.180, bf16[1,64,128,32]{2,1,3,0:T(8,128)(2,1)S(1)} %constant_dynamic-slice_fusion.8), kind=kOutput, calls=%fused_computation.15.clone.1 | convolution fusion | flops 133693440 | bytes 4734848 | tf_op jit(solution)/shard_map/while/body/eval_jaxpr/qab,abd->qd/dot_general | solution.py:65
  183.8 2.5 %fusion.84 = bf16[8,255,32]{1,2,0:T(8,128)(2,1)S(1)} fusion(bf16[8,255,32]{1,2,0:T(8,128)(2,1)S(1)} %get-tuple-element.189, s32[]{:T(128)} %get-tuple-element.188, f32[255,32]{0,1:T(8,128)S(1)} %fusion.83, bf16[255,64,128]{2,1,0:T(8,128)(2,1)S(1)} %get-tuple-element.181, bf16[1,64,128,32]{2,1,3,0:T(8,128)(2,1)S(1)} %constant_dynamic-slice_fusion.8), kind=kOutput, calls=%fused_computation.19.clone.1 | convolution fusion | flops 133701600 | bytes 4767748 | tf_op jit(solution)/shard_map/while/body/eval_jaxpr/qab,abd->qd/dot_general | solution.py:68
  186.3 0.3 fusion.69
  186.9 0.7 fusion.70
  187.8 0.8 add_convert_fusion
  (75 shorter events, 4.4 us)
Async XLA Ops:
  6.5 180.3 %copy-start = (bf16[1024,256]{1,0:T(8,128)(2,1)S(1)}, bf16[1024,256]{1,0:T(8,128)(2,1)}, u32[]{:S(2)}) copy-start(bf16[1024,256]{1,0:T(8,128)(2,1)} %param.30) | copy-start | bytes 1572868
  6.5 73.0 %all-gather.4.cloned.1.call-start = ((), (), s32[]{:S(2)}) async-start(), calls=%async_computation | async-start | bytes 4718592 | tf_op jit(solution)/shard_map/all_gather | solution.py:24
  101.4 84.9 %copy-start.1 = (bf16[255,256]{1,0:T(8,128)(2,1)S(1)}, bf16[255,256]{1,0:T(8,128)(2,1)}, u32[]{:S(2)}) copy-start(bf16[255,256]{1,0:T(8,128)(2,1)} %param.18) | copy-start | bytes 391684
  101.4 84.9 %copy-start.2 = (bf16[256,256]{1,0:T(8,128)(2,1)S(1)}, bf16[256,256]{1,0:T(8,128)(2,1)}, u32[]{:S(2)}) copy-start(bf16[256,256]{1,0:T(8,128)(2,1)} %param.24) | copy-start | bytes 393220
  101.4 84.9 %copy-start.3 = (f32[256]{0:T(256)S(1)}, f32[256]{0:T(256)}, u32[]{:S(2)}) copy-start(f32[256]{0:T(256)} %param.25) | copy-start | bytes 3076
  101.4 85.5 %copy-start.6 = (bf16[256,1024]{1,0:T(8,128)(2,1)S(1)}, bf16[256,1024]{1,0:T(8,128)(2,1)}, u32[]{:S(2)}) copy-start(bf16[256,1024]{1,0:T(8,128)(2,1)} %param.28) | copy-start | bytes 1572868
  101.4 85.5 %copy-start.7 = (f32[1024]{0:T(1024)S(1)}, f32[1024]{0:T(1024)}, u32[]{:S(2)}) copy-start(f32[1024]{0:T(1024)} %param.29) | copy-start | bytes 12292
  101.4 85.5 %copy-start.8 = (f32[256]{0:T(256)S(1)}, f32[256]{0:T(256)}, u32[]{:S(2)}) copy-start(f32[256]{0:T(256)} %param.31) | copy-start | bytes 3076
  101.4 85.5 %copy-start.9 = (f32[256]{0:T(256)S(1)}, f32[256]{0:T(256)}, u32[]{:S(2)}) copy-start(f32[256]{0:T(256)} %param.27) | copy-start | bytes 3076
  101.4 85.5 %copy-start.10 = (f32[256]{0:T(256)S(1)}, f32[256]{0:T(256)}, u32[]{:S(2)}) copy-start(f32[256]{0:T(256)} %param.26) | copy-start | bytes 3076
  101.5 86.3 %copy-start.4 = (f32[256]{0:T(256)S(1)}, f32[256]{0:T(256)}, u32[]{:S(2)}) copy-start(f32[256]{0:T(256)} %param.33) | copy-start | bytes 3076
  101.5 86.3 %copy-start.5 = (f32[256]{0:T(256)S(1)}, f32[256]{0:T(256)}, u32[]{:S(2)}) copy-start(f32[256]{0:T(256)} %param.32) | copy-start | bytes 3076
Sparse Core Ops, SparseCore 0:
  21.9 57.5 all-gather.3
where the time goes:
time: 197 us; the launch traced here: 195 us
  matrix products  74.4 us (38%)
  waiting for transfers between devices  53.2 us (27%)
  local copies, waits for them, and re-layouts  36.6 us (19%)
  blocking collectives  14 us (7%)
  between operations  13.6 us (7%)
  other arithmetic  3.03 us (2%)
    all_gather x1, waiting for transfers between devices, stacked_from(): pieces = lax.all_gather(pieces, axes[k], axis=0, tiled=True)  53.2 us
    dot_general x8, matrix products, one_head(): jnp.einsum('qsa,qsb->qab', group_hits, lane_hits, preferred_element_type=...  31.6 us
    dot_general x8, matrix products, one_head(): jnp.einsum('qab,abd->qd', table_minor, value_one, preferred_element_type=...  20.3 us
    dot_general x8, matrix products, one_head(): jnp.einsum('qab,abd->qd', table_major, value_one, preferred_element_type=...  20.3 us
    unnamed x28, local copies, waits for them, and re-layouts  15.5 us
    all_gather x1, blocking collectives, stacked_from(): pieces = lax.all_gather(pieces, axes[k], axis=0, tiled=True)  14 us
    dynamic_slice x40, local copies, waits for them, and re-layouts, blend_rows(): blended = lax.map(one_head, (place_heads, weight_heads, per_head))  11.1 us
    another operation x1, local copies, waits for them, and re-layouts, joined_along(): pieces.reshape(*dims[:dim], dims[dim] * dims[dim + 1], *dims[dim + 2:])  5.19 us
  transfers between devices with their start and end apart: 1, of which 1 were waited for; matrix products, arithmetic and copies ran while one was open for 2% of the time, Pallas kernels for 0%

commit v1 on v0

v1 whole, which is shorter than its diff:
```python
import jax
import jax.numpy as jnp
from jax import lax
from jax.experimental import pallas as pl
from jax.experimental.pallas import tpu as pltpu
from jax.sharding import Mesh
from jax.sharding import PartitionSpec as P

MESH_ID = pl.DeviceIdType.MESH
DP_BAND = ("dp", "band_0", "band_1")
HEADS = 8
NY, NZ = 4, 8
BANDS = NY * NZ
BAND_ROWS = 255
PAD = 256
LEVEL_ROWS = (6144, 1536, 384, 96)
LEVEL_AT = (0, 6144, 7680, 8064)
STRIDE = (128, 64, 32, 16)
BAND_PART = (192, 48, 12, 3)
BAND_AT = (0, 192, 240, 252)
TOKENS = 8160
POINTS = 16
BF = jnp.bfloat16
F32 = jnp.float32
VM = pltpu.VMEM


def dot(a, b, ca, cb, precision=None):
    return lax.dot_general(
        a, b, (((ca,), (cb,)), ((), ())), preferred_element_type=F32, precision=precision
    )


def onehot(rows, columns, hit):
    r = lax.broadcasted_iota(jnp.int32, (rows, columns), 0)
    c = lax.broadcasted_iota(jnp.int32, (rows, columns), 1)
    return hit(r, c).astype(BF)


def exchange_kernel(
    feat, corner, bil, att, w_value, b_value, table, index, weight,
    send_v, send_i, send_w, sems_out, sems_in, y_out, y_in,
):
    y = lax.axis_index("band_0")
    z = lax.axis_index("band_1")
    barrier = pltpu.get_barrier_semaphore()
    for d in range(1, NZ):
        pl.semaphore_signal(
            barrier, inc=1, device_id={"band_1": lax.rem(z + d, NZ)}, device_id_type=MESH_ID
        )
    for d in range(1, NY):
        pl.semaphore_signal(
            barrier, inc=1, device_id={"band_0": lax.rem(y + d, NY)}, device_id_type=MESH_ID
        )

    values = (dot(feat[...], w_value[...], 1, 0) + b_value[...]).astype(BF)
    eye = onehot(256, 256, lambda r, c: r == c)
    turned = dot(eye, values, 1, 1).astype(BF)
    send_v[:, :, 0:BAND_ROWS] = turned.reshape(HEADS, 32, BAND_ROWS)
    pl.semaphore_wait(barrier, NZ + NY - 2)

    here = y * NZ + z

    def z_copy(kind, src, dst, d):
        t = lax.rem(z + d, NZ)
        slot = here if kind == 0 else z
        return pltpu.make_async_remote_copy(
            src_ref=src.at[t],
            dst_ref=dst.at[slot],
            send_sem=sems_out.at[kind, d],
            recv_sem=sems_in.at[kind, d],
            device_id={"band_1": t},
            device_id_type=MESH_ID,
        )

    v_copies = [z_copy(0, send_v, table, d) for d in range(1, NZ)]
    for c in v_copies:
        c.start()
    table[here] = send_v[z]

    pick = onehot(128, 512, lambda r, c: c == 4 * r)
    ids = corner[...]
    high = (ids // 64).astype(F32).astype(BF)
    low = (ids % 64).astype(F32).astype(BF)
    anchor = (dot(pick, high, 1, 1) * 64.0 + dot(pick, low, 1, 1)).astype(jnp.int32)
    level = (lax.broadcasted_iota(jnp.int32, (128, BAND_ROWS), 0) // 4) % 4
    base = jnp.where(
        level == 0,
        LEVEL_AT[0],
        jnp.where(level == 1, LEVEL_AT[1], jnp.where(level == 2, LEVEL_AT[2], LEVEL_AT[3])),
    )
    send_i[...] = jnp.zeros((HEADS, POINTS, PAD), jnp.int32)
    send_i[:, :, 0:BAND_ROWS] = (anchor + base).reshape(HEADS, POINTS, BAND_ROWS)
    i_copies = [z_copy(1, send_i, index, d) for d in range(1, NZ)]
    for c in i_copies:
        c.start()
    index[z] = send_i[z]

    spread = onehot(128, 512, lambda r, c: c // 4 == r).astype(F32)
    each = dot(att[...], spread, 1, 0, lax.Precision.HIGHEST)
    product = (each * bil[...]).astype(BF)
    eye2 = onehot(512, 512, lambda r, c: r == c)
    send_w[:, :, 0:BAND_ROWS] = dot(eye2, product, 1, 1).astype(BF).reshape(HEADS, 64, BAND_ROWS)
    w_copies = [z_copy(2, send_w, weight, d) for d in range(1, NZ)]
    for c in w_copies:
        c.start()
    weight[z] = send_w[z]

    for c in v_copies:
        c.wait_recv()
    y_copies = []
    part = table.at[pl.ds(y * NZ, NZ)]
    for d in range(1, NY):
        y_copies.append(
            pltpu.make_async_remote_copy(
                src_ref=part,
                dst_ref=part,
                send_sem=y_out.at[d],
                recv_sem=y_in.at[d],
                device_id={"band_0": lax.rem(y + d, NY)},
                device_id_type=MESH_ID,
            )
        )
    for c in y_copies:
        c.start()
    for c in i_copies + w_copies:
        c.wait_recv()
    for c in y_copies:
        c.wait_recv()
    for c in v_copies + i_copies + w_copies + y_copies:
        c.wait_send()


def exchange(feat, corner, bil, att, w_value, b_value):
    sem = pltpu.SemaphoreType.DMA
    return pl.pallas_call(
        exchange_kernel,
        out_shape=(
            jax.ShapeDtypeStruct((BANDS, 32, PAD), BF),
            jax.ShapeDtypeStruct((HEADS, POINTS, PAD), jnp.int32),
            jax.ShapeDtypeStruct((HEADS, 64, PAD), BF),
        ),
        in_specs=[pl.BlockSpec(memory_space=VM)] * 6,
        out_specs=(pl.BlockSpec(memory_space=VM),) * 3,
        scratch_shapes=[
            VM((HEADS, 32, PAD), BF),
            VM((HEADS, POINTS, PAD), jnp.int32),
            VM((HEADS, 64, PAD), BF),
            sem((3, NZ)),
            sem((3, NZ)),
            sem((NY,)),
            sem((NY,)),
        ],
        compiler_params=pltpu.CompilerParams(collective_id=0, has_side_effects=True),
        name="exchange",
    )(feat, corner, bil, att, w_value, b_value)


def build_table(parts, rows, table):
    rep = onehot(32, 128, lambda r, c: c % 32 == r)
    rows[TOKENS : TOKENS + 160, :] = jnp.zeros((160, 128), F32)
    for b in range(BANDS):
        wide = dot(parts[b], rep, 0, 0)
        for at, part, first in zip(LEVEL_AT, BAND_PART, BAND_AT):
            rows[at + b * part : at + (b + 1) * part, :] = wide[first : first + part, :]
    for at, count, stride in zip(LEVEL_AT, LEVEL_ROWS, STRIDE):
        size = min(count, 128)
        lane = lax.broadcasted_iota(jnp.int32, (size, 128), 1)

        def step(i, carry, at=at, size=size, stride=stride, lane=lane):
            k = pl.multiple_of(at + i * size, 8)
            first = rows[pl.ds(k, size), :]
            second = rows[pl.ds(k + 1, size), :]
            third = rows[pl.ds(pl.multiple_of(k + stride, 8), size), :]
            fourth = rows[pl.ds(k + stride + 1, size), :]
            table[pl.ds(k, size), :] = jnp.where(
                lane < 64, jnp.where(lane < 32, first, second), jnp.where(lane < 96, third, fourth)
            )
            return carry

        lax.fori_loop(0, count // size, step, 0)


def blend_kernel(index, weight, parts, out, rows, table, picked, spread, ids, sem):
    def fetch(j):
        return pltpu.make_async_copy(index.at[j], ids, sem)

    fetch(0).start()
    build_table(parts, rows, table)
    widen = onehot(64, POINTS * 128, lambda r, c: c // 32 == r)
    rep = onehot(32, 128, lambda r, c: c % 32 == r)

    def block(j, carry):
        fetch(j).wait()
        spread[...] = dot(weight[j], widen, 0, 0)
        for p in range(POINTS):
            for q in range(PAD):
                picked[p * PAD + q : p * PAD + q + 1, :] = table[pl.ds(ids[p, q], 1), :]

        @pl.when(j < HEADS - 1)
        def _():
            fetch(j + 1).start()

        total = picked[0:PAD, :] * spread[:, 0:128]
        for p in range(1, POINTS):
            total += picked[p * PAD : (p + 1) * PAD, :] * spread[:, p * 128 : (p + 1) * 128]
        major = total.astype(BF)
        minor = (total - major.astype(F32)).astype(BF)
        out[j] = (dot(rep, major, 1, 1) + dot(rep, minor, 1, 1)).astype(BF)
        return carry

    lax.fori_loop(0, HEADS, block, 0)


def blend(index, weight, parts):
    return pl.pallas_call(
        blend_kernel,
        out_shape=jax.ShapeDtypeStruct((HEADS, 32, PAD), BF),
        in_specs=[pl.BlockSpec(memory_space=VM)] * 3,
        out_specs=pl.BlockSpec(memory_space=VM),
        scratch_shapes=[
            VM((TOKENS + 160, 128), F32),
            VM((TOKENS, 128), F32),
            VM((POINTS * PAD, 128), F32),
            VM((PAD, POINTS * 128), F32),
            pltpu.SMEM((POINTS, PAD), jnp.int32),
            pltpu.SemaphoreType.DMA,
        ],
        compiler_params=pltpu.CompilerParams(vmem_limit_bytes=56 << 20),
        name="blend",
    )(index, weight, parts)


def layer_norm(inputs, gain, shift):
    average = jnp.mean(inputs, axis=-1, keepdims=True)
    centred = inputs - average
    variance = jnp.mean(centred * centred, axis=-1, keepdims=True)
    return centred * lax.rsqrt(variance + 1e-05) * gain + shift


def finish_kernel(
    blended, feat, w_out, b_out, gain1, shift1, w_in, b_in, w_ff, b_ff, gain2, shift2,
    out, heads, sem_out, sem_in,
):
    z = lax.axis_index("band_1")
    barrier = pltpu.get_barrier_semaphore()
    for d in range(1, NZ):
        pl.semaphore_signal(
            barrier, inc=1, device_id={"band_1": lax.rem(z + d, NZ)}, device_id_type=MESH_ID
        )
    pl.semaphore_wait(barrier, NZ - 1)
    copies = []
    for d in range(1, NZ):
        t = lax.rem(z + d, NZ)
        copies.append(
            pltpu.make_async_remote_copy(
                src_ref=blended.at[t],
                dst_ref=heads.at[z],
                send_sem=sem_out.at[d],
                recv_sem=sem_in.at[d],
                device_id={"band_1": t},
                device_id_type=MESH_ID,
            )
        )
    for c in copies:
        c.start()
    heads[z] = blended[z]
    for c in copies:
        c.wait_recv()
    sampled = heads[...].reshape(256, PAD)
    attended = dot(sampled, w_out[...], 0, 0)[0:BAND_ROWS] + b_out[...]
    middle = layer_norm(feat[...].astype(F32) + attended, gain1[...], shift1[...]).astype(BF)
    hidden = jnp.maximum(dot(middle, w_in[...], 1, 0) + b_in[...], 0.0).astype(BF)
    result = middle.astype(F32) + dot(hidden, w_ff[...], 1, 0) + b_ff[...]
    out[...] = layer_norm(result, gain2[...], shift2[...]).astype(BF)
    for c in copies:
        c.wait_send()


def finish(blended, feat, *params):
    return pl.pallas_call(
        finish_kernel,
        out_shape=jax.ShapeDtypeStruct((BAND_ROWS, 256), BF),
        in_specs=[pl.BlockSpec(memory_space=VM)] * 12,
        out_specs=pl.BlockSpec(memory_space=VM),
        scratch_shapes=[
            VM((HEADS, 32, PAD), BF),
            pltpu.SemaphoreType.DMA((NZ,)),
            pltpu.SemaphoreType.DMA((NZ,)),
        ],
        compiler_params=pltpu.CompilerParams(collective_id=1, has_side_effects=True),
        name="finish",
    )(blended, feat, *params)


def body(
    features, corners, bilinear, attention, w_value, b_value, w_out, b_out,
    norm1_gain, norm1_bias, w_in, b_in, w_ffout, b_ffout, norm2_gain, norm2_bias,
):
    def row(x):
        return x.reshape(1, -1)

    parts, index, weight = exchange(
        features, corners, bilinear, attention, w_value, row(b_value)
    )
    blended = blend(index, weight, parts)
    return finish(
        blended, features, w_out, row(b_out), row(norm1_gain), row(norm1_bias), w_in, row(b_in),
        w_ffout, row(b_ffout), row(norm2_gain), row(norm2_bias),
    )


def solution(mesh):
    split = Mesh(mesh.devices.reshape(mesh.shape["dp"], NY, NZ), DP_BAND)
    return jax.shard_map(
        body,
        mesh=split,
        in_specs=(P(DP_BAND, None),) * 4 + (P(),) * 12,
        out_specs=P(DP_BAND, None),
        check_vma=False,
    )
```

time: 197 us -> 68.6 us (0.35)
  matrix products: 74.4 us -> 0 us
  Pallas kernels: 0 us -> 66.9 us
  waiting for transfers between devices: 53.2 us -> 0 us
  local copies, waits for them, and re-layouts: 36.6 us -> 1.57 us
  blocking collectives: 14 us -> 0 us
  between operations: 13.6 us -> 0.02 us
  other arithmetic: 3.03 us -> 0 us
    dot_general x27 -> x0, matrix products: 74.4 us -> none  [the longest x8 31.6 us: one_head(): jnp.einsum('qsa,qsb->qab', group_hits, lane_hits, preferred_element_type=...]
    pallas_call x0 -> x3, Pallas kernels: none -> 66.9 us  [the longest x1 30.7 us: blend(): pl.pallas_call(blend_kernel, out_shape=jax.ShapeDtypeStruct((HEADS, 32, P...]
    all_gather x1 -> x0, waiting for transfers between devices: 53.2 us -> none  [stacked_from(): pieces = lax.all_gather(pieces, axes[k], axis=0, tiled=True)]
    all_gather x1 -> x0, blocking collectives: 14 us -> none  [stacked_from(): pieces = lax.all_gather(pieces, axes[k], axis=0, tiled=True)]
    unnamed x28 -> x1, local copies, waits for them, and re-layouts: 15.5 us -> 1.57 us
    dynamic_slice x40 -> x0, local copies, waits for them, and re-layouts: 11.1 us -> none  [blend_rows(): blended = lax.map(one_head, (place_heads, weight_heads, per_head))]
    another operation x1 -> x0, local copies, waits for them, and re-layouts: 5.19 us -> none  [joined_along(): pieces.reshape(*dims[:dim], dims[dim] * dims[dim + 1], *dims[dim + 2:])]
    reshape x1 -> x0, local copies, waits for them, and re-layouts: 4.61 us -> none  [stacked_from(): pieces = pieces.reshape(*held, *shard.shape)]
  transfers between devices with their start and end apart: 1 -> 0, of which waited for: 1 -> 0; matrix products, arithmetic and copies ran while one was open for 2% -> 0% of each run, Pallas kernels for 0% -> 0%
where the time goes in v1:
time: 68.6 us; the launch traced here: 68.5 us
  Pallas kernels  66.9 us (98%)
  local copies, waits for them, and re-layouts  1.57 us (2%)
    pallas_call x1, Pallas kernels, blend(): pl.pallas_call(blend_kernel, out_shape=jax.ShapeDtypeStruct((HEADS, 32, P...  30.7 us
    pallas_call x1, Pallas kernels, exchange(): pl.pallas_call(exchange_kernel, out_shape=(jax.ShapeDtypeStruct((BANDS, 3...  23.7 us
    pallas_call x1, Pallas kernels, finish(): pl.pallas_call(finish_kernel, out_shape=jax.ShapeDtypeStruct((BAND_ROWS,...  12.4 us
    unnamed x1, local copies, waits for them, and re-layouts  1.57 us

profile of v1, /device:TPU:6, one launch (start us, length us, event | category | flops | bytes accessed | tf_op | source)
XLA Modules:
  0.0 68.5 jit_solution(9267056702398002064)
XLA Ops:
  0.0 23.7 %exchange.1 = (bf16[32,32,256]{2,1,0:T(8,128)(2,1)}, s32[8,16,256]{2,1,0:T(8,128)}, bf16[8,64,256]{2,1,0:T(8,128)(2,1)}) custom-call(bf16[255,256]{1,0:T(8,128)(2,1)} %feat.3, s32[255,512]{1,0:T(8,128)} %corner.1, f32[255,512]{1,0:T(8,128)} %bil.1, f32[255,128]{1,0:T(8,128)} %att.1, bf16[256,256]{1,0:T(8,128)(2,1)} %w_value.1, f32[1,256]{1,0:T(1,128)} %bitcast.9), custom_call_target="tpu_custom_call" | custom-call | tf_op jit(solution)/shard_map/exchange/pallas_call | solution.py:136
  23.7 30.7 %blend.1.blended = bf16[8,32,256]{2,1,0:T(8,128)(2,1)} custom-call(s32[8,16,256]{2,1,0:T(8,128)} %get-tuple-element.8.index, bf16[8,64,256]{2,1,0:T(8,128)(2,1)} %get-tuple-element.9.weight, bf16[32,32,256]{2,1,0:T(8,128)(2,1)} %get-tuple-element.10.parts), custom_call_target="tpu_custom_call" | custom-call | tf_op jit(solution)/shard_map/blend/pallas_call | solution.py:216
  54.5 12.4 %finish.1 = bf16[255,256]{1,0:T(8,128)(2,1)} custom-call(bf16[8,32,256]{2,1,0:T(8,128)(2,1)} %blend.1.blended, bf16[255,256]{1,0:T(8,128)(2,1)} %feat.3, bf16[256,256]{1,0:T(8,128)(2,1)} %w_out.1, f32[1,256]{1,0:T(1,128)} %bitcast.10, f32[1,256]{1,0:T(1,128)} %bitcast.11, f32[1,256]{1,0:T(1,128)} %bitcast.12, bf16[256,1024]{1,0:T(8,128)(2,1)} %w_in.1, ...), custom_call_target="tpu_custom_call" | custom-call | tf_op jit(solution)/shard_map/finish/pallas_call | solution.py:281
  66.9 1.6 %copy.18 = bf16[255,256]{1,0:T(8,128)(2,1)} copy(bf16[255,256]{1,0:T(8,128)(2,1)} %finish.1) | data formatting | bytes 261120

commit v2 on v1

v2 whole, which is shorter than its diff:
```python
import jax
import jax.numpy as jnp
from jax import lax
from jax.experimental import pallas as pl
from jax.experimental.pallas import tpu as pltpu
from jax.sharding import Mesh
from jax.sharding import PartitionSpec as P

MESH_ID = pl.DeviceIdType.MESH
DP_BAND = ("dp", "band_0", "band_1")
HEADS = 8
NY, NZ = 4, 8
BANDS = NY * NZ
BAND_ROWS = 255
PAD = 256
LEVEL_ROWS = (6144, 1536, 384, 96)
LEVEL_AT = (0, 6144, 7680, 8064)
STRIDE = (128, 64, 32, 16)
BAND_PART = (192, 48, 12, 3)
BAND_AT = (0, 192, 240, 252)
TOKENS = 8160
POINTS = 16
BF = jnp.bfloat16
F32 = jnp.float32
VM = pltpu.VMEM


def dot(a, b, ca, cb, precision=None):
    return lax.dot_general(
        a, b, (((ca,), (cb,)), ((), ())), preferred_element_type=F32, precision=precision
    )


def onehot(rows, columns, hit):
    r = lax.broadcasted_iota(jnp.int32, (rows, columns), 0)
    c = lax.broadcasted_iota(jnp.int32, (rows, columns), 1)
    return hit(r, c).astype(BF)


def layer_norm(inputs, gain, shift):
    average = jnp.mean(inputs, axis=-1, keepdims=True)
    centred = inputs - average
    variance = jnp.mean(centred * centred, axis=-1, keepdims=True)
    return centred * lax.rsqrt(variance + 1e-05) * gain + shift


def layer_kernel(
    feat_in, corner_in, bil_in, att_in, w_value_in, b_value, w_out_in, b_out, gain1, shift1,
    w_in_in, b_in, w_ff_in, b_ff, gain2, shift2,
    out,
    feat, corner, bil, att, w_value, w_out, w_in, w_ff, turned_ids,
    send_v, send_i, send_w, parts, index, weight,
    rows, table, small, picked_a, picked_b, spread_a, spread_b, side_a, side_b, lanes_a, lanes_b,
    major, minor, done, heads, ids_a, ids_b,
    load_sem, ids_sem, sems_out, sems_in, y_out, y_in,
):
    y = lax.axis_index("band_0")
    z = lax.axis_index("band_1")
    here = y * NZ + z
    barrier = pltpu.get_barrier_semaphore()
    for d in range(1, NZ):
        pl.semaphore_signal(
            barrier, inc=1, device_id={"band_1": lax.rem(z + d, NZ)}, device_id_type=MESH_ID
        )
    for d in range(1, NY):
        pl.semaphore_signal(
            barrier, inc=1, device_id={"band_0": lax.rem(y + d, NY)}, device_id_type=MESH_ID
        )
    loads = [
        pltpu.make_async_copy(src, dst, load_sem.at[i])
        for i, (src, dst) in enumerate(
            (
                (feat_in, feat), (w_value_in, w_value), (corner_in, corner), (att_in, att),
                (bil_in, bil), (w_out_in, w_out), (w_in_in, w_in), (w_ff_in, w_ff),
            )
        )
    ]
    for c in loads:
        c.start()

    def z_copy(kind, src, dst, slot, d, back=False):
        t = lax.rem(z + NZ - d, NZ) if back else lax.rem(z + d, NZ)
        return pltpu.make_async_remote_copy(
            src_ref=src.at[t],
            dst_ref=dst.at[slot],
            send_sem=sems_out.at[kind, d],
            recv_sem=sems_in.at[kind, d],
            device_id={"band_1": t},
            device_id_type=MESH_ID,
        )

    def v_copy(d):
        return z_copy(0, send_v, parts, here, d)

    def i_copy(d):
        return z_copy(1, send_i, index, z, d)

    def w_copy(d):
        return z_copy(2, send_w, weight, z, d)

    def h_copy(d):
        return z_copy(3, done, heads, z, d, back=True)

    loads[0].wait()
    loads[1].wait()
    values = (dot(feat[...], w_value[...], 1, 0) + b_value[...]).astype(BF)
    eye = onehot(256, 256, lambda r, c: r == c)
    turned = dot(eye, values, 1, 1).astype(BF)
    send_v[:, :, 0:BAND_ROWS] = turned.reshape(HEADS, 32, BAND_ROWS)
    pl.semaphore_wait(barrier, NZ + NY - 2)
    for d in range(1, NZ):
        v_copy(d).start()
    parts[here] = send_v[z]

    loads[2].wait()
    turned_ids[0, :, :] = jnp.transpose(corner[0:128, :])
    turned_ids[1, :, 0 : BAND_ROWS - 128] = jnp.transpose(corner[128:BAND_ROWS, :])
    level = (lax.broadcasted_iota(jnp.int32, (128, 128), 0) // 4) % 4
    base = jnp.where(
        level == 0,
        LEVEL_AT[0],
        jnp.where(level == 1, LEVEL_AT[1], jnp.where(level == 2, LEVEL_AT[2], LEVEL_AT[3])),
    )
    used = lax.broadcasted_iota(jnp.int32, (128, 128), 1) < BAND_ROWS - 128
    left = turned_ids[0, pl.ds(0, 128, stride=4), :] + base
    right = jnp.where(used, turned_ids[1, pl.ds(0, 128, stride=4), :] + base, 0)
    send_i[:, :, 0:128] = left.reshape(HEADS, POINTS, 128)
    send_i[:, :, 128:256] = right.reshape(HEADS, POINTS, 128)
    for d in range(1, NZ):
        i_copy(d).start()
    index[z] = send_i[z]

    loads[3].wait()
    loads[4].wait()
    repeat = onehot(128, 512, lambda r, c: c // 4 == r)
    whole = att[...]
    first = whole.astype(BF)
    rest = whole - first.astype(F32)
    second = rest.astype(BF)
    third = (rest - second.astype(F32)).astype(BF)
    each = dot(first, repeat, 1, 0) + dot(second, repeat, 1, 0) + dot(third, repeat, 1, 0)
    product = (each * bil[...]).astype(BF)
    eye2 = onehot(512, 512, lambda r, c: r == c)
    send_w[:, :, 0:BAND_ROWS] = dot(eye2, product, 1, 1).astype(BF).reshape(HEADS, 64, BAND_ROWS)
    for d in range(1, NZ):
        w_copy(d).start()
    weight[z] = send_w[z]

    for d in range(1, NZ):
        v_copy(d).wait_recv()
    part = parts.at[pl.ds(y * NZ, NZ)]
    y_copies = [
        pltpu.make_async_remote_copy(
            src_ref=part,
            dst_ref=part,
            send_sem=y_out.at[d],
            recv_sem=y_in.at[d],
            device_id={"band_0": lax.rem(y + d, NY)},
            device_id_type=MESH_ID,
        )
        for d in range(1, NY)
    ]
    for c in y_copies:
        c.start()
    for c in y_copies:
        c.wait_recv()

    rows[TOKENS : TOKENS + 160, :] = jnp.zeros((160, 128), F32)
    rep = onehot(32, 128, lambda r, c: c % 32 == r)
    for b in range(BANDS):
        wide = dot(parts[b], rep, 0, 0)
        for at, count, begin in zip(LEVEL_AT, BAND_PART, BAND_AT):
            rows[at + b * count : at + (b + 1) * count, :] = wide[begin : begin + count, :]
    for at, count, stride in zip(LEVEL_AT[:2], LEVEL_ROWS[:2], STRIDE[:2]):
        lane = lax.broadcasted_iota(jnp.int32, (128, 128), 1)

        def four(i, carry, at=at, stride=stride, lane=lane):
            k = pl.multiple_of(at + i * 128, 8)
            c0 = rows[pl.ds(k, 128), :]
            c1 = rows[pl.ds(k + 1, 128), :]
            c2 = rows[pl.ds(pl.multiple_of(k + stride, 8), 128), :]
            c3 = rows[pl.ds(k + stride + 1, 128), :]
            table[pl.ds(k, 128), :] = jnp.where(
                lane < 64, jnp.where(lane < 32, c0, c1), jnp.where(lane < 96, c2, c3)
            )
            return carry

        lax.fori_loop(0, count // 128, four, 0)
    pick = onehot(32, 128, lambda r, c: r == c)
    small[...] = dot(pick, rows[LEVEL_AT[2] : LEVEL_AT[2] + 512, :].astype(BF), 1, 1)

    widen = onehot(32, 8 * 128, lambda r, c: c // 32 == r)
    set_a = (picked_a, spread_a, side_a, lanes_a, ids_a, 0)
    set_b = (picked_b, spread_b, side_b, lanes_b, ids_b, 1)

    def owner(d):
        return lax.rem(z + NZ - d, NZ)

    def fetch(d, bufs):
        return pltpu.make_async_copy(
            index.at[owner(d), pl.ds(0, 8)], bufs[4], ids_sem.at[bufs[5]]
        )

    def lanes_part(j, side, lanes, r):
        half, i = r % 2, r // 2
        at = slice(half * 128, half * 128 + 128)
        sums = [lanes[v * 8 : v * 8 + 8, at] for v in range(4)]
        for point, level in ((i, 2), (i + 4, 3)):
            place = index[j, 8 + point : 9 + point, at] - LEVEL_AT[2]
            for c, off in enumerate((0, 1, STRIDE[level], STRIDE[level] + 1)):
                spot = jnp.broadcast_to(place + off, (8, 128))
                lane = spot & 127
                group = spot >> 7
                w = jnp.broadcast_to(side[point * 4 + c : point * 4 + c + 1, at], (8, 128))
                for v in range(4):

                    def take(g):
                        window = small[v * 8 : v * 8 + 8, g * 128 : g * 128 + 128]
                        return jnp.take_along_axis(
                            window, lane, axis=1, mode="promise_in_bounds"
                        )

                    if level == 3:
                        got = take(3)
                    else:
                        got = jnp.where(
                            group == 0, take(0), jnp.where(group == 1, take(1), take(2))
                        )
                    sums[v] = sums[v] + got * w
        for v in range(4):
            lanes[v * 8 : v * 8 + 8, at] = sums[v]

    def add_up(bufs, c):
        picked, spread = bufs[0], bufs[1]
        total = None
        for r in range(8):
            term = (
                picked[r * PAD + c * 32 : r * PAD + c * 32 + 32, :]
                * spread[c * 32 : c * 32 + 32, r * 128 : r * 128 + 128]
            )
            total = term if total is None else total + term
        top = total.astype(BF)
        major[c * 32 : c * 32 + 32, :] = top
        minor[c * 32 : c * 32 + 32, :] = (total - top.astype(F32)).astype(BF)

    def close(d, bufs):
        done[owner(d)] = (
            dot(rep, major[...], 1, 1) + dot(rep, minor[...], 1, 1) + bufs[3][...]
        ).astype(BF)

    def send_back(d):
        @pl.when(d == 0)
        def _():
            heads[z] = done[z]

        @pl.when(d > 0)
        def _():
            h_copy(d).start()

    def stage(d, bufs, other, last):
        picked, spread, side, lanes, ids, _ = bufs
        j = owner(d)
        if not last:
            i_copy(d + 1).wait_recv()
            fetch(d + 1, other).start()
        else:

            @pl.when(d < NZ - 1)
            def _():
                i_copy(d + 1).wait_recv()
                fetch(d + 1, other).start()

        @pl.when(d > 0)
        def _():
            w_copy(d).wait_recv()

        fetch(d, bufs).wait()
        spread[...] = dot(weight[j, 0:32, :], widen, 0, 0)
        side[...] = weight[j, 32:64, :].astype(F32)
        lanes[...] = jnp.zeros((32, PAD), F32)
        for r in range(8):

            @pl.when(d > -1 - r)
            def _(r=r):
                for q in range(PAD):
                    picked[r * PAD + q : r * PAD + q + 1, :] = table[pl.ds(ids[r, q], 1), :]
                lanes_part(j, side, lanes, r)
                add_up(other, r)

    fetch(0, set_a).start()

    def pair(i, carry):
        d = 2 * i
        stage(d, set_a, set_b, False)

        @pl.when(i > 0)
        def _():
            close(d - 1, set_b)
            send_back(d - 1)

        stage(d + 1, set_b, set_a, True)
        close(d, set_a)
        send_back(d)
        return carry

    lax.fori_loop(0, NZ // 2, pair, 0)
    for c in range(8):
        add_up(set_b, c)
    close(NZ - 1, set_b)
    send_back(NZ - 1)

    for c in loads[5:]:
        c.wait()
    for d in range(1, NZ):
        h_copy(d).wait_recv()
    sampled = heads[...].reshape(256, PAD)
    attended = dot(sampled, w_out[...], 0, 0)[0:BAND_ROWS] + b_out[...]
    middle = layer_norm(feat[...].astype(F32) + attended, gain1[...], shift1[...]).astype(BF)
    hidden = jnp.maximum(dot(middle, w_in[...], 1, 0) + b_in[...], 0.0).astype(BF)
    result = middle.astype(F32) + dot(hidden, w_ff[...], 1, 0) + b_ff[...]
    out[...] = layer_norm(result, gain2[...], shift2[...]).astype(BF)
    for d in range(1, NZ):
        for c in (v_copy(d), i_copy(d), w_copy(d), h_copy(d)):
            c.wait_send()
    for c in y_copies:
        c.wait_send()


def body(
    features, corners, bilinear, attention, w_value, b_value, w_out, b_out,
    norm1_gain, norm1_bias, w_in, b_in, w_ffout, b_ffout, norm2_gain, norm2_bias,
):
    def row(x):
        return x.reshape(1, -1)

    def like(x):
        return VM(x.shape, x.dtype)

    dma = pltpu.SemaphoreType.DMA
    big = pl.BlockSpec(memory_space=pl.ANY)
    vec = pl.BlockSpec(memory_space=VM)
    return pl.pallas_call(
        layer_kernel,
        out_shape=jax.ShapeDtypeStruct((BAND_ROWS, 256), BF),
        in_specs=[big] * 5 + [vec, big, vec, vec, vec, big, vec, big, vec, vec, vec],
        out_specs=vec,
        scratch_shapes=[
            like(features), like(corners), like(bilinear), like(attention), like(w_value),
            like(w_out), like(w_in), like(w_ffout),
            VM((2, 512, 128), jnp.int32),
            VM((HEADS, 32, PAD), BF),
            VM((HEADS, POINTS, PAD), jnp.int32),
            VM((HEADS, 64, PAD), BF),
            VM((BANDS, 32, PAD), BF),
            VM((HEADS, POINTS, PAD), jnp.int32),
            VM((HEADS, 64, PAD), BF),
            VM((TOKENS + 160, 128), F32),
            VM((LEVEL_AT[2], 128), F32),
            VM((32, 512), F32),
            VM((8 * PAD, 128), F32),
            VM((8 * PAD, 128), F32),
            VM((PAD, 8 * 128), F32),
            VM((PAD, 8 * 128), F32),
            VM((32, PAD), F32),
            VM((32, PAD), F32),
            VM((32, PAD), F32),
            VM((32, PAD), F32),
            VM((PAD, 128), BF),
            VM((PAD, 128), BF),
            VM((HEADS, 32, PAD), BF),
            VM((HEADS, 32, PAD), BF),
            pltpu.SMEM((8, PAD), jnp.int32),
            pltpu.SMEM((8, PAD), jnp.int32),
            dma((8,)),
            dma((2,)),
            dma((4, NZ)),
            dma((4, NZ)),
            dma((NY,)),
            dma((NY,)),
        ],
        compiler_params=pltpu.CompilerParams(
            collective_id=0, has_side_effects=True, vmem_limit_bytes=60 << 20
        ),
        name="layer",
    )(
        features, corners, bilinear, attention, w_value, row(b_value), w_out, row(b_out),
        row(norm1_gain), row(norm1_bias), w_in, row(b_in), w_ffout, row(b_ffout),
        row(norm2_gain), row(norm2_bias),
    )


def solution(mesh):
    split = Mesh(mesh.devices.reshape(mesh.shape["dp"], NY, NZ), DP_BAND)
    return jax.shard_map(
        body,
        mesh=split,
        in_specs=(P(DP_BAND, None),) * 4 + (P(),) * 12,
        out_specs=P(DP_BAND, None),
        check_vma=False,
    )
```

time: 68.6 us -> 51.6 us (0.75)
  Pallas kernels: 66.9 us -> 49.9 us
    pallas_call x3 -> x1, Pallas kernels: 66.9 us -> 49.9 us  [body(): pl.pallas_call(layer_kernel, out_shape=jax.ShapeDtypeStruct((BAND_ROWS, 2...]
where the time goes in v2:
time: 51.6 us; the launch traced here: 51.4 us
  Pallas kernels  49.9 us (97%)
  local copies, waits for them, and re-layouts  1.57 us (3%)
    pallas_call x1, Pallas kernels, body(): pl.pallas_call(layer_kernel, out_shape=jax.ShapeDtypeStruct((BAND_ROWS, 2...  49.9 us
    unnamed x1, local copies, waits for them, and re-layouts  1.57 us

profile of v2, /device:TPU:6, one launch (start us, length us, event | category | flops | bytes accessed | tf_op | source)
XLA Modules:
  0.0 51.4 jit_solution(5970128940091731047)
XLA Ops:
  0.0 49.9 %layer.1 = bf16[255,256]{1,0:T(8,128)(2,1)} custom-call(bf16[255,256]{1,0:T(8,128)(2,1)} %feat_in.1, s32[255,512]{1,0:T(8,128)} %corner_in.1, f32[255,512]{1,0:T(8,128)} %bil_in.1, f32[255,128]{1,0:T(8,128)} %att_in.1, bf16[256,256]{1,0:T(8,128)(2,1)} %w_value_in.1, f32[1,256]{1,0:T(1,128)} %bitcast.9, bf16[256,256]{1,0:T(8,128)(2,1)} %w_out_in.1, ...), custom_call_target="tpu_custom_call" | custom-call | tf_op jit(solution)/shard_map/layer/pallas_call | solution.py:342
  49.9 1.6 %copy.18 = bf16[255,256]{1,0:T(8,128)(2,1)} copy(bf16[255,256]{1,0:T(8,128)(2,1)} %layer.1) | data formatting | bytes 261120

commit v3 on v2

v3 whole, which is shorter than its diff:
```python
import jax
import jax.numpy as jnp
from jax import lax
from jax.experimental import pallas as pl
from jax.experimental.pallas import tpu as pltpu
from jax.sharding import Mesh
from jax.sharding import PartitionSpec as P

MESH_ID = pl.DeviceIdType.MESH
DP_BAND = ("dp", "band_0", "band_1")
HEADS = 8
NY, NZ = 4, 8
BANDS = NY * NZ
BAND_ROWS = 255
PAD = 256
LEVEL_ROWS = (6144, 1536, 384, 96)
LEVEL_AT = (0, 6144, 7680, 8064)
STRIDE = (128, 64, 32, 16)
BAND_PART = (192, 48, 12, 3)
BAND_AT = (0, 192, 240, 252)
TOKENS = 8160
POINTS = 16
BF = jnp.bfloat16
F32 = jnp.float32
VM = pltpu.VMEM


def dot(a, b, ca, cb, precision=None):
    return lax.dot_general(
        a, b, (((ca,), (cb,)), ((), ())), preferred_element_type=F32, precision=precision
    )


def onehot(rows, columns, hit):
    r = lax.broadcasted_iota(jnp.int32, (rows, columns), 0)
    c = lax.broadcasted_iota(jnp.int32, (rows, columns), 1)
    return hit(r, c).astype(BF)


def layer_norm(inputs, gain, shift):
    average = jnp.mean(inputs, axis=-1, keepdims=True)
    centred = inputs - average
    variance = jnp.mean(centred * centred, axis=-1, keepdims=True)
    return centred * lax.rsqrt(variance + 1e-05) * gain + shift


def layer_kernel(
    feat_in, corner_in, bil_in, att_in, w_value_in, b_value_in, w_out_in, b_out_in, gain1_in, shift1_in,
    w_in_in, b_in_in, w_ff_in, b_ff_in, gain2_in, shift2_in,
    out,
    feat, corner, bil, att, w_value, b_value, w_out, b_out, gain1, shift1, w_in, b_in, w_ff, b_ff,
    gain2, shift2, turned_ids,
    send_v, send_s, send_i, send_w, parts, smalls, index, weight, near_i, near_w, near_sum, coarse,
    rows, table, spread_a, spread_b, major_a, major_b, minor_a, minor_b, done, heads, ids_a, ids_b,
    load_sem, ids_sem, sems_out, sems_in, y_out, y_in,
):
    y = lax.axis_index("band_0")
    z = lax.axis_index("band_1")
    here = y * NZ + z
    barrier = pltpu.get_barrier_semaphore()
    for d in range(1, NZ):
        pl.semaphore_signal(
            barrier, inc=1, device_id={"band_1": lax.rem(z + d, NZ)}, device_id_type=MESH_ID
        )
    for d in (1, NY - 1):
        pl.semaphore_signal(
            barrier, inc=1, device_id={"band_0": lax.rem(y + d, NY)}, device_id_type=MESH_ID
        )
    loads = [
        pltpu.make_async_copy(src, dst, load_sem.at[i])
        for i, (src, dst) in enumerate(
            (
                (feat_in, feat), (w_value_in, w_value), (b_value_in, b_value), (corner_in, corner),
                (att_in, att), (bil_in, bil), (w_out_in, w_out), (b_out_in, b_out),
                (gain1_in, gain1), (shift1_in, shift1), (w_in_in, w_in), (b_in_in, b_in),
                (w_ff_in, w_ff), (b_ff_in, b_ff), (gain2_in, gain2), (shift2_in, shift2),
            )
        )
    ]
    for c in loads[0:3]:
        c.start()

    def z_copy(kind, src, dst, slot, d, back=False):
        t = lax.rem(z + NZ - d, NZ) if back else lax.rem(z + d, NZ)
        return pltpu.make_async_remote_copy(
            src_ref=src if src is send_s else src.at[t],
            dst_ref=dst.at[slot],
            send_sem=sems_out.at[kind, d],
            recv_sem=sems_in.at[kind, d],
            device_id={"band_1": t},
            device_id_type=MESH_ID,
        )

    def v_copy(d):
        return z_copy(0, send_v, parts, here, d)

    def i_copy(d):
        return z_copy(1, send_i, index, z, d)

    def w_copy(d):
        return z_copy(2, send_w, weight, z, d)

    def h_copy(d):
        return z_copy(3, done, heads, z, d, back=True)

    def s_copy(d):
        return z_copy(4, send_s, smalls, here, d)

    def y_copy(kind, ref, leg):
        step = (1, 1, NY - 1, NY - 1, 1, NY - 1)[leg]
        column = (y, y, y, y, lax.rem(y + NY - 1, NY), lax.rem(y + 1, NY))[leg]
        half = (0, 1, 1, 0, 0, 1)[leg]
        piece = ref.at[pl.ds(column * NZ + half * (NZ // 2), NZ // 2)]
        return pltpu.make_async_remote_copy(
            src_ref=piece,
            dst_ref=piece,
            send_sem=y_out.at[kind, leg],
            recv_sem=y_in.at[kind, leg],
            device_id={"band_0": lax.rem(y + step, NY)},
            device_id_type=MESH_ID,
        )

    for c in loads[0:3]:
        c.wait()
    for c in loads[3:]:
        c.start()
    values = (dot(feat[...], w_value[...], 1, 0) + b_value[...]).astype(BF)
    eye = onehot(256, 256, lambda r, c: r == c)
    turned = dot(eye, values, 1, 1).astype(BF)
    send_s[...] = jnp.zeros((16, 256), BF)
    send_s[0:15, :] = values[BAND_AT[2] : BAND_ROWS, :]
    send_v[:, :, 0:BAND_ROWS] = turned.reshape(HEADS, 32, BAND_ROWS)
    pl.semaphore_wait(barrier, NZ + 1)
    for d in range(1, NZ):
        s_copy(d).start()
    for d in range(1, NZ):
        v_copy(d).start()
    parts[here] = send_v[z]
    smalls[here] = send_s[...]

    loads[3].wait()
    turned_ids[0, :, :] = jnp.transpose(corner[0:128, :])
    turned_ids[1, :, 0 : BAND_ROWS - 128] = jnp.transpose(corner[128:BAND_ROWS, :])
    level = (lax.broadcasted_iota(jnp.int32, (128, 128), 0) // 4) % 4
    base = jnp.where(
        level == 0, LEVEL_AT[0], jnp.where(level == 1, LEVEL_AT[1], jnp.where(level == 2, 0, 384))
    )
    used = lax.broadcasted_iota(jnp.int32, (128, 128), 1) < BAND_ROWS - 128
    left = turned_ids[0, pl.ds(0, 128, stride=4), :] + base
    right = jnp.where(used, turned_ids[1, pl.ds(0, 128, stride=4), :] + base, 0)
    for at, side in ((0, left), (128, right)):
        side = side.reshape(HEADS, POINTS, 128)
        send_i[:, :, at : at + 128] = side[:, 0:8]
        near_i[:, :, at : at + 128] = side[:, 8:16]
    for d in range(1, NZ):
        i_copy(d).start()
    index[z] = send_i[z]

    loads[4].wait()
    loads[5].wait()
    repeat = onehot(128, 512, lambda r, c: c // 4 == r)
    whole = att[...]
    first = whole.astype(BF)
    rest = whole - first.astype(F32)
    second = rest.astype(BF)
    third = (rest - second.astype(F32)).astype(BF)
    each = dot(first, repeat, 1, 0) + dot(second, repeat, 1, 0) + dot(third, repeat, 1, 0)
    product = (each * bil[...]).astype(BF)
    eye2 = onehot(512, 512, lambda r, c: r == c)
    turned_w = dot(eye2, product, 1, 1).reshape(HEADS, 64, BAND_ROWS)
    send_w[:, :, 0:BAND_ROWS] = turned_w[:, 0:32].astype(BF)
    near_w[:, :, 0:BAND_ROWS] = turned_w[:, 32:64]
    for d in range(1, NZ):
        w_copy(d).start()
    weight[z] = send_w[z]

    widen = onehot(32, 8 * 128, lambda r, c: c // 32 == r)
    sub = lax.broadcasted_iota(jnp.int32, (8, 128), 0)
    set_a = (spread_a, major_a, minor_a, ids_a, 0)
    set_b = (spread_b, major_b, minor_b, ids_b, 1)

    def owner(d):
        return lax.rem(z + 2 * NZ - d, NZ)

    def fetch(d, bufs):
        return pltpu.make_async_copy(index.at[owner(d)], bufs[3], ids_sem.at[bufs[4]])

    spread_a[...] = dot(weight[z], widen, 0, 0)
    major_b[...] = jnp.zeros((PAD, 128), BF)
    minor_b[...] = jnp.zeros((PAD, 128), BF)
    fetch(0, set_a).start()

    for d in range(1, NZ):
        s_copy(d).wait_recv()
    for leg in range(4):
        y_copy(1, smalls, leg).start()
    rep = onehot(32, 128, lambda r, c: c % 32 == r)
    for d in range(1, NZ):
        v_copy(d).wait_recv()
    for leg in (0, 2):
        y_copy(0, parts, leg).start()

    def add_rows(column):
        for i in range(NZ):
            b = column * NZ + i
            wide = dot(parts[b], rep, 0, 0)
            for at, count, begin in zip(LEVEL_AT[:2], BAND_PART[:2], BAND_AT[:2]):
                rows[pl.ds(pl.multiple_of(at + b * count, 16), count), :] = wide[
                    begin : begin + count, :
                ]

    rows[LEVEL_AT[2] : LEVEL_AT[2] + 128, :] = jnp.zeros((128, 128), F32)
    add_rows(y)
    place = lax.broadcasted_iota(jnp.int32, (512, 512), 0)
    spot = lax.broadcasted_iota(jnp.int32, (512, 512), 1)
    inner = place % 16
    goal = jnp.where(
        inner < 12,
        place // 16 * 12 + inner,
        jnp.where(inner < 15, 384 + place // 16 * 3 + inner - 12, -1),
    )
    to_map = (goal == spot).astype(BF)

    for came, leg in ((0, 4), (2, 5)):
        y_copy(1, smalls, came).wait_recv()
        y_copy(1, smalls, leg).start()
    for leg in (1, 3):
        y_copy(0, parts, leg).start()
    for came, leg in ((0, 4), (2, 5)):
        y_copy(0, parts, came).wait_recv()
        y_copy(0, parts, leg).start()
    for came in (1, 3, 4, 5):
        y_copy(1, smalls, came).wait_recv()
    coarse[...] = dot(smalls[...].reshape(512, 256), to_map, 0, 0).reshape(HEADS, 32, 512)

    def near_head(h, carry):
        for half in range(2):
            at = slice(half * 128, half * 128 + 128)
            sums = [jnp.zeros((8, 128), F32) for _ in range(4)]
            for point in range(8):
                stride = STRIDE[2 + point // 4]
                anchor = near_i[h, point : point + 1, at]
                for c, off in enumerate((0, 1, stride, stride + 1)):
                    spot = jnp.broadcast_to(anchor + off, (8, 128))
                    lane = spot & 127
                    group = spot >> 7
                    w = jnp.broadcast_to(near_w[h, point * 4 + c : point * 4 + c + 1, at], (8, 128))
                    for v in range(4):

                        def take(g):
                            window = coarse[h, v * 8 : v * 8 + 8, g * 128 : g * 128 + 128]
                            return jnp.take_along_axis(
                                window, lane, axis=1, mode="promise_in_bounds"
                            )

                        if point >= 4:
                            got = take(3)
                        else:
                            got = jnp.where(
                                group == 0, take(0), jnp.where(group == 1, take(1), take(2))
                            )
                        sums[v] = sums[v] + got * w
            near_sum[h, :, at] = jnp.concatenate(sums, axis=0)
        return carry

    lax.fori_loop(0, 4, near_head, 0)
    for came in (1, 3):
        y_copy(0, parts, came).wait_recv()
    add_rows(lax.rem(y + 1, NY))
    add_rows(lax.rem(y + 3, NY))
    for came in (4, 5):
        y_copy(0, parts, came).wait_recv()
    add_rows(lax.rem(y + 2, NY))

    for at, count, stride in zip(LEVEL_AT[:2], LEVEL_ROWS[:2], STRIDE[:2]):
        lane = lax.broadcasted_iota(jnp.int32, (128, 128), 1)

        def four(i, carry, at=at, stride=stride, lane=lane):
            k = pl.multiple_of(at + i * 128, 8)
            c0 = rows[pl.ds(k, 128), :]
            c1 = rows[pl.ds(k + 1, 128), :]
            c2 = rows[pl.ds(pl.multiple_of(k + stride, 8), 128), :]
            c3 = rows[pl.ds(k + stride + 1, 128), :]
            table[pl.ds(k, 128), :] = jnp.where(
                lane < 64, jnp.where(lane < 32, c0, c1), jnp.where(lane < 96, c2, c3)
            )
            return carry

        lax.fori_loop(0, count // 128, four, 0)

    def close(d, bufs):
        done[owner(d)] = (dot(rep, bufs[1][...], 1, 1) + dot(rep, bufs[2][...], 1, 1)).astype(BF)

    def send_back(d):
        @pl.when(d == 0)
        def _():
            heads[z] = done[z]

        @pl.when(d > 0)
        def _():
            h_copy(d).start()

    def stage(d, bufs, other):
        spread, major, minor, ids, _ = bufs

        @pl.when(d < NZ - 1)
        def _():
            i_copy(d + 1).wait_recv()
            fetch(d + 1, other).start()
            w_copy(d + 1).wait_recv()

        fetch(d, bufs).wait()
        other[0][...] = dot(weight[owner(d + 1)], widen, 0, 0)
        for chunk in range(8):
            total = []
            for q0 in range(chunk * 32, chunk * 32 + 32, 8):
                acc = None
                for r in range(8):
                    got = None
                    for k in range(8):
                        one = jnp.broadcast_to(table[pl.ds(ids[r, q0 + k], 1), :], (8, 128))
                        got = one if got is None else jnp.where(sub == k, one, got)
                    term = got * spread[q0 : q0 + 8, r * 128 : r * 128 + 128]
                    acc = term if acc is None else acc + term
                total.append(acc)
            total = jnp.concatenate(total, axis=0)
            top = total.astype(BF)
            major[chunk * 32 : chunk * 32 + 32, :] = top
            minor[chunk * 32 : chunk * 32 + 32, :] = (total - top.astype(F32)).astype(BF)
        close(d - 1, other)

    def pair(i, carry):
        d = 2 * i
        stage(d, set_a, set_b)

        @pl.when(i > 0)
        def _():
            send_back(d - 1)

        stage(d + 1, set_b, set_a)
        send_back(d)
        return carry

    lax.fori_loop(0, NZ // 2, pair, 0)
    close(NZ - 1, set_b)
    send_back(NZ - 1)

    lax.fori_loop(4, HEADS, near_head, 0)
    for c in loads[6:]:
        c.wait()
    for d in range(1, NZ):
        h_copy(d).wait_recv()
    sampled = (
        heads[...].reshape(256, PAD).astype(F32) + near_sum[...].reshape(256, PAD)
    ).astype(BF)
    attended = dot(sampled, w_out[...], 0, 0)[0:BAND_ROWS] + b_out[...]
    middle = layer_norm(feat[...].astype(F32) + attended, gain1[...], shift1[...]).astype(BF)
    hidden = jnp.maximum(dot(middle, w_in[...], 1, 0) + b_in[...], 0.0).astype(BF)
    result = middle.astype(F32) + dot(hidden, w_ff[...], 1, 0) + b_ff[...]
    out[...] = layer_norm(result, gain2[...], shift2[...]).astype(BF)
    for d in range(1, NZ):
        for c in (v_copy(d), i_copy(d), w_copy(d), h_copy(d), s_copy(d)):
            c.wait_send()
    for leg in range(6):
        y_copy(0, parts, leg).wait_send()
        y_copy(1, smalls, leg).wait_send()


def body(
    features, corners, bilinear, attention, w_value, b_value, w_out, b_out,
    norm1_gain, norm1_bias, w_in, b_in, w_ffout, b_ffout, norm2_gain, norm2_bias,
):
    def row(x):
        return x.reshape(1, -1)

    def like(x):
        return VM(x.shape, x.dtype)

    def flat(n):
        return VM((1, n), F32)

    dma = pltpu.SemaphoreType.DMA
    vec = pl.BlockSpec(memory_space=VM)
    return pl.pallas_call(
        layer_kernel,
        out_shape=jax.ShapeDtypeStruct((BAND_ROWS, 256), BF),
        in_specs=[pl.BlockSpec(memory_space=pl.ANY)] * 16,
        out_specs=vec,
        scratch_shapes=[
            like(features), like(corners), like(bilinear), like(attention), like(w_value), flat(256),
            like(w_out), flat(256), flat(256), flat(256), like(w_in), flat(1024), like(w_ffout),
            flat(256), flat(256), flat(256),
            VM((2, 512, 128), jnp.int32),
            VM((HEADS, 32, PAD), BF),
            VM((16, 256), BF),
            VM((HEADS, 8, PAD), jnp.int32),
            VM((HEADS, 32, PAD), BF),
            VM((BANDS, 32, PAD), BF),
            VM((BANDS, 16, 256), BF),
            VM((HEADS, 8, PAD), jnp.int32),
            VM((HEADS, 32, PAD), BF),
            VM((HEADS, 8, PAD), jnp.int32),
            VM((HEADS, 32, PAD), F32),
            VM((HEADS, 32, PAD), F32),
            VM((HEADS, 32, 512), F32),
            VM((LEVEL_AT[2] + 128, 128), F32),
            VM((LEVEL_AT[2], 128), F32),
            VM((PAD, 8 * 128), F32),
            VM((PAD, 8 * 128), F32),
            VM((PAD, 128), BF),
            VM((PAD, 128), BF),
            VM((PAD, 128), BF),
            VM((PAD, 128), BF),
            VM((HEADS, 32, PAD), BF),
            VM((HEADS, 32, PAD), BF),
            pltpu.SMEM((8, PAD), jnp.int32),
            pltpu.SMEM((8, PAD), jnp.int32),
            dma((16,)),
            dma((2,)),
            dma((5, NZ)),
            dma((5, NZ)),
            dma((2, 6)),
            dma((2, 6)),
        ],
        compiler_params=pltpu.CompilerParams(
            collective_id=0, has_side_effects=True, vmem_limit_bytes=60 << 20
        ),
        name="layer",
    )(
        features, corners, bilinear, attention, w_value, row(b_value), w_out, row(b_out),
        row(norm1_gain), row(norm1_bias), w_in, row(b_in), w_ffout, row(b_ffout),
        row(norm2_gain), row(norm2_bias),
    )


def solution(mesh):
    split = Mesh(mesh.devices.reshape(mesh.shape["dp"], NY, NZ), DP_BAND)
    return jax.shard_map(
        body,
        mesh=split,
        in_specs=(P(DP_BAND, None),) * 4 + (P(),) * 12,
        out_specs=P(DP_BAND, None),
        check_vma=False,
    )
```

time: 51.6 us -> 45.6 us (0.88)
  Pallas kernels: 49.9 us -> 43.9 us
    pallas_call x1, Pallas kernels: 49.9 us -> 43.9 us  [body(): pl.pallas_call(layer_kernel, out_shape=jax.ShapeDtypeStruct((BAND_ROWS, 2...]
where the time goes in v3:
time: 45.6 us; the launch traced here: 45.5 us
  Pallas kernels  43.9 us (96%)
  local copies, waits for them, and re-layouts  1.57 us (3%)
    pallas_call x1, Pallas kernels, body(): pl.pallas_call(layer_kernel, out_shape=jax.ShapeDtypeStruct((BAND_ROWS, 2...  43.9 us
    unnamed x1, local copies, waits for them, and re-layouts  1.57 us

profile of v3, /device:TPU:6, one launch (start us, length us, event | category | flops | bytes accessed | tf_op | source)
XLA Modules:
  0.0 45.5 jit_solution(7731990710836951637)
XLA Ops:
  0.0 43.9 %layer.1 = bf16[255,256]{1,0:T(8,128)(2,1)} custom-call(bf16[255,256]{1,0:T(8,128)(2,1)} %feat_in.1, s32[255,512]{1,0:T(8,128)} %corner_in.1, f32[255,512]{1,0:T(8,128)} %bil_in.1, f32[255,128]{1,0:T(8,128)} %att_in.1, bf16[256,256]{1,0:T(8,128)(2,1)} %w_value_in.1, f32[1,256]{1,0:T(1,128)} %bitcast.9, bf16[256,256]{1,0:T(8,128)(2,1)} %w_out_in.1, ...), custom_call_target="tpu_custom_call" | custom-call | tf_op jit(solution)/shard_map/layer/pallas_call | solution.py:384
  43.9 1.6 %copy.18 = bf16[255,256]{1,0:T(8,128)(2,1)} copy(bf16[255,256]{1,0:T(8,128)(2,1)} %layer.1) | data formatting | bytes 261120

commit v4 on v3

--- a/solution.py
+++ b/solution.py
@@ -20,6 +20,7 @@
 BAND_AT = (0, 192, 240, 252)
 TOKENS = 8160
 POINTS = 16
+FAR_FIRST = (4, 3, 5, 2, 6, 1, 7)
 BF = jnp.bfloat16
 F32 = jnp.float32
 VM = pltpu.VMEM
@@ -131,9 +132,9 @@
     send_s[0:15, :] = values[BAND_AT[2] : BAND_ROWS, :]
     send_v[:, :, 0:BAND_ROWS] = turned.reshape(HEADS, 32, BAND_ROWS)
     pl.semaphore_wait(barrier, NZ + 1)
-    for d in range(1, NZ):
+    for d in FAR_FIRST:
         s_copy(d).start()
-    for d in range(1, NZ):
+    for d in FAR_FIRST:
         v_copy(d).start()
     parts[here] = send_v[z]
     smalls[here] = send_s[...]
@@ -152,7 +153,7 @@
         side = side.reshape(HEADS, POINTS, 128)
         send_i[:, :, at : at + 128] = side[:, 0:8]
         near_i[:, :, at : at + 128] = side[:, 8:16]
-    for d in range(1, NZ):
+    for d in FAR_FIRST:
         i_copy(d).start()
     index[z] = send_i[z]
 
@@ -170,7 +171,7 @@
     turned_w = dot(eye2, product, 1, 1).reshape(HEADS, 64, BAND_ROWS)
     send_w[:, :, 0:BAND_ROWS] = turned_w[:, 0:32].astype(BF)
     near_w[:, :, 0:BAND_ROWS] = turned_w[:, 32:64]
-    for d in range(1, NZ):
+    for d in FAR_FIRST:
         w_copy(d).start()
     weight[z] = send_w[z]
 
@@ -263,7 +264,7 @@
             near_sum[h, :, at] = jnp.concatenate(sums, axis=0)
         return carry
 
-    lax.fori_loop(0, 4, near_head, 0)
+    lax.fori_loop(0, 3, near_head, 0)
     for came in (1, 3):
         y_copy(0, parts, came).wait_recv()
     add_rows(lax.rem(y + 1, NY))
@@ -345,7 +346,7 @@
     close(NZ - 1, set_b)
     send_back(NZ - 1)
 
-    lax.fori_loop(4, HEADS, near_head, 0)
+    lax.fori_loop(3, HEADS, near_head, 0)
     for c in loads[6:]:
         c.wait()
     for d in range(1, NZ):

time: 45.6 us -> 43.8 us (0.961)
  Pallas kernels: 43.9 us -> 42.1 us
    pallas_call x1, Pallas kernels: 43.9 us -> 42.1 us  [body(): pl.pallas_call(layer_kernel, out_shape=jax.ShapeDtypeStruct((BAND_ROWS, 2...]
where the time goes in v4:
time: 43.8 us; the launch traced here: 43.7 us
  Pallas kernels  42.1 us (96%)
  local copies, waits for them, and re-layouts  1.57 us (4%)
    pallas_call x1, Pallas kernels, body(): pl.pallas_call(layer_kernel, out_shape=jax.ShapeDtypeStruct((BAND_ROWS, 2...  42.1 us
    unnamed x1, local copies, waits for them, and re-layouts  1.57 us

profile of v4, /device:TPU:6, one launch (start us, length us, event | category | flops | bytes accessed | tf_op | source)
XLA Modules:
  0.0 43.7 jit_solution(7908919977799854286)
XLA Ops:
  0.0 42.1 %layer.1 = bf16[255,256]{1,0:T(8,128)(2,1)} custom-call(bf16[255,256]{1,0:T(8,128)(2,1)} %feat_in.1, s32[255,512]{1,0:T(8,128)} %corner_in.1, f32[255,512]{1,0:T(8,128)} %bil_in.1, f32[255,128]{1,0:T(8,128)} %att_in.1, bf16[256,256]{1,0:T(8,128)(2,1)} %w_value_in.1, f32[1,256]{1,0:T(1,128)} %bitcast.9, bf16[256,256]{1,0:T(8,128)(2,1)} %w_out_in.1, ...), custom_call_target="tpu_custom_call" | custom-call | tf_op jit(solution)/shard_map/layer/pallas_call | solution.py:385
  42.1 1.6 %copy.18 = bf16[255,256]{1,0:T(8,128)(2,1)} copy(bf16[255,256]{1,0:T(8,128)(2,1)} %layer.1) | data formatting | bytes 261120

commit v5 on v4

--- a/solution.py
+++ b/solution.py
@@ -43,6 +43,22 @@
     centred = inputs - average
     variance = jnp.mean(centred * centred, axis=-1, keepdims=True)
     return centred * lax.rsqrt(variance + 1e-05) * gain + shift
+
+
+def lanes_of(window, lane):
+    return lax.gather(
+        window,
+        lane[..., None],
+        lax.GatherDimensionNumbers(
+            offset_dims=(),
+            collapsed_slice_dims=(1,),
+            start_index_map=(1,),
+            operand_batching_dims=(0,),
+            start_indices_batching_dims=(0,),
+        ),
+        slice_sizes=(1, 1),
+        mode=lax.GatherScatterMode.PROMISE_IN_BOUNDS,
+    )
 
 
 def layer_kernel(
@@ -107,11 +123,22 @@
     def s_copy(d):
         return z_copy(4, send_s, smalls, here, d)
 
-    def y_copy(kind, ref, leg):
-        step = (1, 1, NY - 1, NY - 1, 1, NY - 1)[leg]
-        column = (y, y, y, y, lax.rem(y + NY - 1, NY), lax.rem(y + 1, NY))[leg]
-        half = (0, 1, 1, 0, 0, 1)[leg]
-        piece = ref.at[pl.ds(column * NZ + half * (NZ // 2), NZ // 2)]
+    above, below = lax.rem(y + 1, NY), lax.rem(y + NY - 1, NY)
+    legs = (
+        (
+            (1, y, 0, 4), (1, y, 4, 4), (NY - 1, y, 4, 4), (NY - 1, y, 0, 4),
+            (1, below, 0, 4), (NY - 1, above, 4, 4),
+        ),
+        (
+            (1, y, 0, 2), (1, y, 2, 2), (NY - 1, y, 4, 2), (NY - 1, y, 6, 2),
+            (1, y, 4, 4), (NY - 1, y, 0, 4),
+            (1, below, 0, 2), (NY - 1, above, 4, 2), (1, below, 2, 2), (NY - 1, above, 6, 2),
+        ),
+    )
+
+    def y_copy(kind, leg):
+        step, column, begin, count = legs[kind][leg]
+        piece = (smalls, parts)[kind].at[pl.ds(column * NZ + begin, count)]
         return pltpu.make_async_remote_copy(
             src_ref=piece,
             dst_ref=piece,
@@ -181,25 +208,23 @@
     set_b = (spread_b, major_b, minor_b, ids_b, 1)
 
     def owner(d):
-        return lax.rem(z + 2 * NZ - d, NZ)
+        return lax.rem(z + 2 * NZ - 1 - d, NZ)
 
     def fetch(d, bufs):
         return pltpu.make_async_copy(index.at[owner(d)], bufs[3], ids_sem.at[bufs[4]])
 
-    spread_a[...] = dot(weight[z], widen, 0, 0)
     major_b[...] = jnp.zeros((PAD, 128), BF)
     minor_b[...] = jnp.zeros((PAD, 128), BF)
-    fetch(0, set_a).start()
 
     for d in range(1, NZ):
         s_copy(d).wait_recv()
     for leg in range(4):
-        y_copy(1, smalls, leg).start()
+        y_copy(0, leg).start()
     rep = onehot(32, 128, lambda r, c: c % 32 == r)
     for d in range(1, NZ):
         v_copy(d).wait_recv()
-    for leg in (0, 2):
-        y_copy(0, parts, leg).start()
+    for leg in (0, 2, 1, 3):
+        y_copy(1, leg).start()
 
     def add_rows(column):
         for i in range(NZ):
@@ -209,6 +234,25 @@
                 rows[pl.ds(pl.multiple_of(at + b * count, 16), count), :] = wide[
                     begin : begin + count, :
                 ]
+
+    def four(start, count, level):
+        stride = STRIDE[level]
+        lane = lax.broadcasted_iota(jnp.int32, (128, 128), 1)
+
+        def chunk(i, carry):
+            k = (start + i) * 128
+            k = jnp.where(k >= LEVEL_ROWS[level], k - LEVEL_ROWS[level], k) + LEVEL_AT[level]
+            k = pl.multiple_of(k, 128)
+            c0 = rows[pl.ds(k, 128), :]
+            c1 = rows[pl.ds(k + 1, 128), :]
+            c2 = rows[pl.ds(pl.multiple_of(k + stride, 8), 128), :]
+            c3 = rows[pl.ds(k + stride + 1, 128), :]
+            table[pl.ds(k, 128), :] = jnp.where(
+                lane < 64, jnp.where(lane < 32, c0, c1), jnp.where(lane < 96, c2, c3)
+            )
+            return carry
+
+        lax.fori_loop(0, count, chunk, 0)
 
     rows[LEVEL_AT[2] : LEVEL_AT[2] + 128, :] = jnp.zeros((128, 128), F32)
     add_rows(y)
@@ -223,92 +267,86 @@
     to_map = (goal == spot).astype(BF)
 
     for came, leg in ((0, 4), (2, 5)):
-        y_copy(1, smalls, came).wait_recv()
-        y_copy(1, smalls, leg).start()
-    for leg in (1, 3):
-        y_copy(0, parts, leg).start()
-    for came, leg in ((0, 4), (2, 5)):
-        y_copy(0, parts, came).wait_recv()
-        y_copy(0, parts, leg).start()
+        y_copy(0, came).wait_recv()
+        y_copy(0, leg).start()
+    for leg in (4, 5):
+        y_copy(1, leg).start()
+    for came, leg in ((0, 6), (2, 7), (1, 8), (3, 9)):
+        y_copy(1, came).wait_recv()
+        y_copy(1, leg).start()
+    i_copy(1).wait_recv()
+    fetch(0, set_a).start()
+    w_copy(1).wait_recv()
+    spread_a[...] = dot(weight[owner(0)], widen, 0, 0)
     for came in (1, 3, 4, 5):
-        y_copy(1, smalls, came).wait_recv()
-    coarse[...] = dot(smalls[...].reshape(512, 256), to_map, 0, 0).reshape(HEADS, 32, 512)
+        y_copy(0, came).wait_recv()
+    coarse[...] = dot(smalls[...].reshape(512, 256), to_map, 0, 0).astype(BF).reshape(
+        HEADS, 32, 512
+    )
 
     def near_head(h, carry):
         for half in range(2):
             at = slice(half * 128, half * 128 + 128)
-            sums = [jnp.zeros((8, 128), F32) for _ in range(4)]
+            sums = [jnp.zeros((16, 128), F32) for _ in range(2)]
             for point in range(8):
                 stride = STRIDE[2 + point // 4]
-                anchor = near_i[h, point : point + 1, at]
+                anchor = jnp.broadcast_to(near_i[h, point : point + 1, at], (16, 128)).astype(
+                    jnp.int16
+                )
                 for c, off in enumerate((0, 1, stride, stride + 1)):
-                    spot = jnp.broadcast_to(anchor + off, (8, 128))
-                    lane = spot & 127
-                    group = spot >> 7
-                    w = jnp.broadcast_to(near_w[h, point * 4 + c : point * 4 + c + 1, at], (8, 128))
-                    for v in range(4):
+                    spot = anchor + jnp.int16(off)
+                    lane = spot & jnp.int16(127)
+                    w = jnp.broadcast_to(
+                        near_w[h, point * 4 + c : point * 4 + c + 1, at], (16, 128)
+                    )
+                    for v in range(2):
 
                         def take(g):
-                            window = coarse[h, v * 8 : v * 8 + 8, g * 128 : g * 128 + 128]
-                            return jnp.take_along_axis(
-                                window, lane, axis=1, mode="promise_in_bounds"
+                            return lanes_of(
+                                coarse[h, v * 16 : v * 16 + 16, g * 128 : g * 128 + 128], lane
                             )
 
                         if point >= 4:
                             got = take(3)
                         else:
                             got = jnp.where(
-                                group == 0, take(0), jnp.where(group == 1, take(1), take(2))
+                                spot < 128, take(0), jnp.where(spot < 256, take(1), take(2))
                             )
-                        sums[v] = sums[v] + got * w
+                        sums[v] = sums[v] + got.astype(F32) * w
             near_sum[h, :, at] = jnp.concatenate(sums, axis=0)
         return carry
 
-    lax.fori_loop(0, 3, near_head, 0)
-    for came in (1, 3):
-        y_copy(0, parts, came).wait_recv()
+    lax.fori_loop(0, 2, near_head, 0)
+    for came in (4, 5):
+        y_copy(1, came).wait_recv()
     add_rows(lax.rem(y + 1, NY))
     add_rows(lax.rem(y + 3, NY))
-    for came in (4, 5):
-        y_copy(0, parts, came).wait_recv()
+    four(lax.rem(y + 3, NY) * 12, 34, 0)
+    four(lax.rem(y + 3, NY) * 3, 8, 1)
+    for came in (6, 7, 8, 9):
+        y_copy(1, came).wait_recv()
     add_rows(lax.rem(y + 2, NY))
 
-    for at, count, stride in zip(LEVEL_AT[:2], LEVEL_ROWS[:2], STRIDE[:2]):
-        lane = lax.broadcasted_iota(jnp.int32, (128, 128), 1)
-
-        def four(i, carry, at=at, stride=stride, lane=lane):
-            k = pl.multiple_of(at + i * 128, 8)
-            c0 = rows[pl.ds(k, 128), :]
-            c1 = rows[pl.ds(k + 1, 128), :]
-            c2 = rows[pl.ds(pl.multiple_of(k + stride, 8), 128), :]
-            c3 = rows[pl.ds(k + stride + 1, 128), :]
-            table[pl.ds(k, 128), :] = jnp.where(
-                lane < 64, jnp.where(lane < 32, c0, c1), jnp.where(lane < 96, c2, c3)
-            )
-            return carry
-
-        lax.fori_loop(0, count // 128, four, 0)
+    four(lax.rem(y + 1, NY) * 12 + 10, 14, 0)
+    four(lax.rem(y + 1, NY) * 3 + 2, 4, 1)
 
     def close(d, bufs):
         done[owner(d)] = (dot(rep, bufs[1][...], 1, 1) + dot(rep, bufs[2][...], 1, 1)).astype(BF)
 
     def send_back(d):
-        @pl.when(d == 0)
-        def _():
-            heads[z] = done[z]
-
-        @pl.when(d > 0)
-        def _():
-            h_copy(d).start()
+        h_copy(d + 1).start()
 
     def stage(d, bufs, other):
         spread, major, minor, ids, _ = bufs
 
+        @pl.when(d < NZ - 2)
+        def _():
+            i_copy(d + 2).wait_recv()
+            w_copy(d + 2).wait_recv()
+
         @pl.when(d < NZ - 1)
         def _():
-            i_copy(d + 1).wait_recv()
             fetch(d + 1, other).start()
-            w_copy(d + 1).wait_recv()
 
         fetch(d, bufs).wait()
         other[0][...] = dot(weight[owner(d + 1)], widen, 0, 0)
@@ -344,9 +382,9 @@
 
     lax.fori_loop(0, NZ // 2, pair, 0)
     close(NZ - 1, set_b)
-    send_back(NZ - 1)
-
-    lax.fori_loop(3, HEADS, near_head, 0)
+    heads[z] = done[z]
+
+    lax.fori_loop(2, HEADS, near_head, 0)
     for c in loads[6:]:
         c.wait()
     for d in range(1, NZ):
@@ -362,9 +400,9 @@
     for d in range(1, NZ):
         for c in (v_copy(d), i_copy(d), w_copy(d), h_copy(d), s_copy(d)):
             c.wait_send()
-    for leg in range(6):
-        y_copy(0, parts, leg).wait_send()
-        y_copy(1, smalls, leg).wait_send()
+    for kind in range(2):
+        for leg in range(len(legs[kind])):
+            y_copy(kind, leg).wait_send()
 
 
 def body(
@@ -403,7 +441,7 @@
             VM((HEADS, 8, PAD), jnp.int32),
             VM((HEADS, 32, PAD), F32),
             VM((HEADS, 32, PAD), F32),
-            VM((HEADS, 32, 512), F32),
+            VM((HEADS, 32, 512), BF),
             VM((LEVEL_AT[2] + 128, 128), F32),
             VM((LEVEL_AT[2], 128), F32),
             VM((PAD, 8 * 128), F32),
@@ -420,8 +458,8 @@
             dma((2,)),
             dma((5, NZ)),
             dma((5, NZ)),
-            dma((2, 6)),
-            dma((2, 6)),
+            dma((2, 10)),
+            dma((2, 10)),
         ],
         compiler_params=pltpu.CompilerParams(
             collective_id=0, has_side_effects=True, vmem_limit_bytes=60 << 20

time: 43.8 us -> 50.5 us (1.15)
  Pallas kernels: 42.1 us -> 48.8 us
    pallas_call x1, Pallas kernels: 42.1 us -> 48.8 us  [body(): pl.pallas_call(layer_kernel, out_shape=jax.ShapeDtypeStruct((BAND_ROWS, 2...]
where the time goes in v5:
time: 50.5 us; the launch traced here: 50.4 us
  Pallas kernels  48.8 us (97%)
  local copies, waits for them, and re-layouts  1.57 us (3%)
    pallas_call x1, Pallas kernels, body(): pl.pallas_call(layer_kernel, out_shape=jax.ShapeDtypeStruct((BAND_ROWS, 2...  48.8 us
    unnamed x1, local copies, waits for them, and re-layouts  1.57 us

profile of v5, /device:TPU:6, one launch (start us, length us, event | category | flops | bytes accessed | tf_op | source)
XLA Modules:
  0.0 50.4 jit_solution(10247031054399119141)
XLA Ops:
  0.0 48.8 %layer.1 = bf16[255,256]{1,0:T(8,128)(2,1)} custom-call(bf16[255,256]{1,0:T(8,128)(2,1)} %feat_in.1, s32[255,512]{1,0:T(8,128)} %corner_in.1, f32[255,512]{1,0:T(8,128)} %bil_in.1, f32[255,128]{1,0:T(8,128)} %att_in.1, bf16[256,256]{1,0:T(8,128)(2,1)} %w_value_in.1, f32[1,256]{1,0:T(1,128)} %bitcast.9, bf16[256,256]{1,0:T(8,128)(2,1)} %w_out_in.1, ...), custom_call_target="tpu_custom_call" | custom-call | tf_op jit(solution)/shard_map/layer/pallas_call | solution.py:423
  48.8 1.6 %copy.18 = bf16[255,256]{1,0:T(8,128)(2,1)} copy(bf16[255,256]{1,0:T(8,128)(2,1)} %layer.1) | data formatting | bytes 261120

commit v6 on v5

--- a/solution.py
+++ b/solution.py
@@ -349,24 +349,27 @@
             fetch(d + 1, other).start()
 
         fetch(d, bufs).wait()
-        other[0][...] = dot(weight[owner(d + 1)], widen, 0, 0)
-        for chunk in range(8):
-            total = []
-            for q0 in range(chunk * 32, chunk * 32 + 32, 8):
-                acc = None
-                for r in range(8):
-                    got = None
-                    for k in range(8):
-                        one = jnp.broadcast_to(table[pl.ds(ids[r, q0 + k], 1), :], (8, 128))
-                        got = one if got is None else jnp.where(sub == k, one, got)
-                    term = got * spread[q0 : q0 + 8, r * 128 : r * 128 + 128]
-                    acc = term if acc is None else acc + term
-                total.append(acc)
-            total = jnp.concatenate(total, axis=0)
-            top = total.astype(BF)
-            major[chunk * 32 : chunk * 32 + 32, :] = top
-            minor[chunk * 32 : chunk * 32 + 32, :] = (total - top.astype(F32)).astype(BF)
-        close(d - 1, other)
+
+        @pl.when(here + d > -1)
+        def _():
+            other[0][...] = dot(weight[owner(d + 1)], widen, 0, 0)
+            for chunk in range(8):
+                total = []
+                for q0 in range(chunk * 32, chunk * 32 + 32, 8):
+                    acc = None
+                    for r in range(8):
+                        got = None
+                        for k in range(8):
+                            one = jnp.broadcast_to(table[pl.ds(ids[r, q0 + k], 1), :], (8, 128))
+                            got = one if got is None else jnp.where(sub == k, one, got)
+                        term = got * spread[q0 : q0 + 8, r * 128 : r * 128 + 128]
+                        acc = term if acc is None else acc + term
+                    total.append(acc)
+                total = jnp.concatenate(total, axis=0)
+                top = total.astype(BF)
+                major[chunk * 32 : chunk * 32 + 32, :] = top
+                minor[chunk * 32 : chunk * 32 + 32, :] = (total - top.astype(F32)).astype(BF)
+            close(d - 1, other)
 
     def pair(i, carry):
         d = 2 * i

time: 50.5 us -> 42.3 us (0.84)
  Pallas kernels: 48.8 us -> 40.6 us
    pallas_call x1, Pallas kernels: 48.8 us -> 40.6 us  [body(): pl.pallas_call(layer_kernel, out_shape=jax.ShapeDtypeStruct((BAND_ROWS, 2...]
where the time goes in v6:
time: 42.3 us; the launch traced here: 42.2 us
  Pallas kernels  40.6 us (96%)
  local copies, waits for them, and re-layouts  1.57 us (4%)
    pallas_call x1, Pallas kernels, body(): pl.pallas_call(layer_kernel, out_shape=jax.ShapeDtypeStruct((BAND_ROWS, 2...  40.6 us
    unnamed x1, local copies, waits for them, and re-layouts  1.57 us

profile of v6, /device:TPU:6, one launch (start us, length us, event | category | flops | bytes accessed | tf_op | source)
XLA Modules:
  0.0 42.2 jit_solution(2706938000689086502)
XLA Ops:
  0.0 40.6 %layer.1 = bf16[255,256]{1,0:T(8,128)(2,1)} custom-call(bf16[255,256]{1,0:T(8,128)(2,1)} %feat_in.1, s32[255,512]{1,0:T(8,128)} %corner_in.1, f32[255,512]{1,0:T(8,128)} %bil_in.1, f32[255,128]{1,0:T(8,128)} %att_in.1, bf16[256,256]{1,0:T(8,128)(2,1)} %w_value_in.1, f32[1,256]{1,0:T(1,128)} %bitcast.9, bf16[256,256]{1,0:T(8,128)(2,1)} %w_out_in.1, ...), custom_call_target="tpu_custom_call" | custom-call | tf_op jit(solution)/shard_map/layer/pallas_call | solution.py:426
  40.6 1.6 %copy.18 = bf16[255,256]{1,0:T(8,128)(2,1)} copy(bf16[255,256]{1,0:T(8,128)(2,1)} %layer.1) | data formatting | bytes 261120

commit v7 on v6

--- a/solution.py
+++ b/solution.py
@@ -316,7 +316,7 @@
             near_sum[h, :, at] = jnp.concatenate(sums, axis=0)
         return carry
 
-    lax.fori_loop(0, 2, near_head, 0)
+    lax.fori_loop(0, 1, near_head, 0)
     for came in (4, 5):
         y_copy(1, came).wait_recv()
     add_rows(lax.rem(y + 1, NY))
@@ -387,7 +387,7 @@
     close(NZ - 1, set_b)
     heads[z] = done[z]
 
-    lax.fori_loop(2, HEADS, near_head, 0)
+    lax.fori_loop(1, HEADS, near_head, 0)
     for c in loads[6:]:
         c.wait()
     for d in range(1, NZ):

time: 42.3 us -> 42 us (level)
  no operation moved by 1% of the time
where the time goes in v7:
time: 42 us; the launch traced here: 41.9 us
  Pallas kernels  40.3 us (96%)
  local copies, waits for them, and re-layouts  1.57 us (4%)
    pallas_call x1, Pallas kernels, body(): pl.pallas_call(layer_kernel, out_shape=jax.ShapeDtypeStruct((BAND_ROWS, 2...  40.3 us
    unnamed x1, local copies, waits for them, and re-layouts  1.57 us

profile of v7, /device:TPU:6, one launch (start us, length us, event | category | flops | bytes accessed | tf_op | source)
XLA Modules:
  0.0 41.9 jit_solution(10604555264342928938)
XLA Ops:
  0.0 40.3 %layer.1 = bf16[255,256]{1,0:T(8,128)(2,1)} custom-call(bf16[255,256]{1,0:T(8,128)(2,1)} %feat_in.1, s32[255,512]{1,0:T(8,128)} %corner_in.1, f32[255,512]{1,0:T(8,128)} %bil_in.1, f32[255,128]{1,0:T(8,128)} %att_in.1, bf16[256,256]{1,0:T(8,128)(2,1)} %w_value_in.1, f32[1,256]{1,0:T(1,128)} %bitcast.9, bf16[256,256]{1,0:T(8,128)(2,1)} %w_out_in.1, ...), custom_call_target="tpu_custom_call" | custom-call | tf_op jit(solution)/shard_map/layer/pallas_call | solution.py:426
  40.3 1.6 %copy.18 = bf16[255,256]{1,0:T(8,128)(2,1)} copy(bf16[255,256]{1,0:T(8,128)(2,1)} %layer.1) | data formatting | bytes 261120
